TPU v7x, 32 devices: a whole 2x2x4 slice. The times are simulated.
32 devices in a mesh: shard: 4 (over x, core), context: 4 (over z), tensor: 2 (over y).
Axes of the slice: x: 2, y: 2, z: 4, core: 2. Of those that a mesh axis runs over, the one named last changes fastest.
Arguments:
- hidden_in: bfloat16 [2048, 1536], P(('shard', 'context')), may hold values from -6 to 6
- segment_ids: int32 [4, 512], P('shard'), may hold values from 0 to 2, never falling along the last dimension, each value on 1 to 256 neighbouring positions
- attn_gain: bfloat16 [1536], P(('shard', 'context')), may hold values from 0.25 to 1.75
- qkv_weight: bfloat16 [1536, 2048], P(('shard', 'context'), 'tensor'), may hold values from -0.15625 to 0.15625
- qkv_bias: bfloat16 [16, 128], P('tensor', ('shard', 'context')), may hold values from -3 to 3
- out_weight: bfloat16 [1536, 1536], P('tensor', ('shard', 'context')), may hold values from -0.625 to 0.625
- ffn_gain: bfloat16 [1536], P(('shard', 'context')), may hold values from 0.25 to 1.75
- gate_weight: bfloat16 [1536, 8960], P(('shard', 'context'), 'tensor'), may hold values from -0.15625 to 0.15625
- up_weight: bfloat16 [1536, 8960], P(('shard', 'context'), 'tensor'), may hold values from -0.15625 to 0.15625
- down_weight: bfloat16 [8960, 1536], P('tensor', ('shard', 'context')), may hold values from -0.0625 to 0.0625
- out_cotangent: bfloat16 [2048, 1536], P(('shard', 'context')), may hold values from -6 to 6
Outputs:
- block_out: bfloat16 [2048, 1536], P(('shard', 'context'))
- input_grad: float32 [2048, 1536], P(('shard', 'context'))
- attn_gain_grad: float32 [1536], P(('shard', 'context'))
- qkv_weight_grad: float32 [1536, 2048], P(('shard', 'context'), 'tensor')
- qkv_bias_grad: float32 [16, 128], P('tensor', ('shard', 'context'))
- out_weight_grad: float32 [1536, 1536], P('tensor', ('shard', 'context'))
- ffn_gain_grad: float32 [1536], P(('shard', 'context'))
- gate_weight_grad: float32 [1536, 8960], P(('shard', 'context'), 'tensor')
- up_weight_grad: float32 [1536, 8960], P(('shard', 'context'), 'tensor')
- down_weight_grad: float32 [8960, 1536], P('tensor', ('shard', 'context'))
Inputs may be any that keep to these rules, and one draw needn't show every extreme that they name: `segment_ids`: in every group the sequence numbers start at 0 and never fall; a sequence has at most 256 tokens, and one sequence of each group has exactly 256.
All inputs are finite; a program needn't handle non-finite values.
Results may differ from a plain program's by a relative error of at most 0.018.
Values may be sent and summed in bfloat16 or wider, within the bound.
A program may use at most 256 MiB of HBM per device.

v0:
```python
import jax
import jax.numpy as jnp
from jax import lax
from jax.sharding import PartitionSpec as P

H = 12
KVH = 2
HD = 128


EPSILON = 1e-06
THETA = 1000000.0


def contract_last(left, right):
    return lax.dot_general(
        left, right, (((1,), (1,)), ((), ())), preferred_element_type=jnp.float32
    )


def contract_first(left, right):
    return lax.dot_general(
        left, right, (((0,), (0,)), ((), ())), preferred_element_type=jnp.float32
    )


def norm_forward(values, gain):
    factor = lax.rsqrt(jnp.mean(values * values, axis=1, keepdims=True) + EPSILON)
    unit = values * factor
    return ((unit * gain.astype(jnp.float32)).astype(jnp.bfloat16), unit, factor)


def norm_backward(grad_out, unit, factor, gain):
    gain_grad = jnp.sum(grad_out * unit, axis=0)
    scaled = grad_out * gain.astype(jnp.float32)
    return (gain_grad, factor * (scaled - unit * jnp.mean(scaled * unit, axis=1, keepdims=True)))


def rotary_tables(positions, head_dim):
    half = head_dim // 2
    freqs = THETA ** (-(2.0 * jnp.arange(half, dtype=jnp.float32)) / head_dim)
    angles = positions.astype(jnp.float32)[:, None] * freqs[None, :]
    return (jnp.cos(angles), jnp.sin(angles))


def rotate_pairs(values, cosine, sine):
    half = values.shape[-1] // 2
    first = values[..., :half]
    second = values[..., half:]
    cos_b = cosine[:, None, :]
    sin_b = sine[:, None, :]
    return jnp.concatenate(
        [first * cos_b - second * sin_b, second * cos_b + first * sin_b], axis=-1
    )


def unrotate_pairs(grads, cosine, sine):
    half = grads.shape[-1] // 2
    first = grads[..., :half]
    second = grads[..., half:]
    cos_b = cosine[:, None, :]
    sin_b = sine[:, None, :]
    return jnp.concatenate(
        [first * cos_b + second * sin_b, second * cos_b - first * sin_b], axis=-1
    )


def head_forward(query, keys, values, allowed, scale):
    scores = jnp.where(allowed, contract_last(query, keys) * scale, -1e30)
    peak = jnp.max(scores, axis=1, keepdims=True)
    total = jnp.sum(jnp.exp(scores - peak), axis=1, keepdims=True)
    lse = peak + jnp.log(total)
    probs = jnp.exp(scores - lse).astype(jnp.bfloat16)
    out = jnp.dot(probs, values, preferred_element_type=jnp.float32).astype(jnp.bfloat16)
    return (out, lse[:, 0])


def head_backward(query, keys, values, allowed, scale, out, lse, grad):
    scores = jnp.where(allowed, contract_last(query, keys) * scale, -1e30)
    probs = jnp.exp(scores - lse[:, None])
    dprob = contract_last(grad, values)
    delta = jnp.sum(grad.astype(jnp.float32) * out.astype(jnp.float32), axis=1, keepdims=True)
    dscore = (probs * (dprob - delta)).astype(jnp.bfloat16)
    dquery = jnp.dot(dscore, keys, preferred_element_type=jnp.float32) * scale
    dkeys = contract_first(dscore, query) * scale
    dvalues = contract_first(probs.astype(jnp.bfloat16), grad)
    return (dquery, dkeys, dvalues)


def group_attention(queries, keys, values, allowed, scale):

    def one_kv(items):
        group_q, key_one, value_one = items
        return lax.map(
            lambda query: head_forward(query, key_one, value_one, allowed, scale), group_q
        )

    return lax.map(one_kv, (queries, keys, values))


def group_attention_back(queries, keys, values, allowed, scale, outs, lses, grads):

    def one_kv(items):
        group_q, key_one, value_one, out_g, lse_g, grad_g = items
        dquery, dkeys, dvalues = lax.map(
            lambda inner: head_backward(
                inner[0], key_one, value_one, allowed, scale, inner[1], inner[2], inner[3]
            ),
            (group_q, out_g, lse_g, grad_g),
        )
        return (dquery, jnp.sum(dkeys, axis=0), jnp.sum(dvalues, axis=0))

    return lax.map(one_kv, (queries, keys, values, outs, lses, grads))


def local(
    hidden_in,
    segment_ids,
    attn_gain,
    qkv_weight,
    qkv_bias,
    out_weight,
    ffn_gain,
    gate_weight,
    up_weight,
    down_weight,
    out_cotangent,
):
    rows = hidden_in.shape[0]
    parts = lax.axis_size("tensor")
    local_heads = H // parts
    local_kv = KVH // parts
    repeat = H // KVH
    scale = HD ** (-0.5)
    block_index = lax.axis_index("context")
    seg_all = segment_ids[0]
    group_rows = seg_all.shape[0]
    first_row = block_index * rows
    index_all = jnp.arange(group_rows, dtype=jnp.int32)
    index_local = first_row + jnp.arange(rows, dtype=jnp.int32)
    seg_local = lax.dynamic_slice_in_dim(seg_all, first_row, rows)
    earlier = jnp.sum((seg_all[None, :] < seg_local[:, None]).astype(jnp.int32), axis=1)
    positions = index_local - earlier
    allowed = (seg_local[:, None] == seg_all[None, :]) & (
        index_local[:, None] >= index_all[None, :]
    )
    cosine, sine = rotary_tables(positions, HD)
    attn_set = (
        lax.all_gather(attn_gain, ("shard", "context"), axis=0, tiled=True),
        lax.all_gather(qkv_weight, ("shard", "context"), axis=0, tiled=True),
        lax.all_gather(qkv_bias, ("shard", "context"), axis=1, tiled=True),
        lax.all_gather(out_weight, ("shard", "context"), axis=1, tiled=True),
    )
    gain_one, qkv_full, bias_full, out_full = attn_set
    hidden_f = hidden_in.astype(jnp.float32)
    normed1, unit1, factor1 = norm_forward(hidden_f, gain_one)
    projected = jnp.dot(normed1, qkv_full, preferred_element_type=jnp.float32) + bias_full.reshape(
        -1
    ).astype(jnp.float32)
    query_f = projected[:, : local_heads * HD].reshape(rows, local_heads, HD)
    keys_f = projected[:, local_heads * HD : (local_heads + local_kv) * HD].reshape(
        rows, local_kv, HD
    )
    values_local = projected[:, (local_heads + local_kv) * HD :].astype(jnp.bfloat16)
    query_b = rotate_pairs(query_f, cosine, sine).astype(jnp.bfloat16)
    keys_local = (
        rotate_pairs(keys_f, cosine, sine).astype(jnp.bfloat16).reshape(rows, local_kv * HD)
    )
    keys_all, values_all = (
        lax.all_gather(keys_local, "context", axis=0, tiled=True),
        lax.all_gather(values_local, "context", axis=0, tiled=True),
    )
    query_g = jnp.transpose(query_b.reshape(rows, local_kv, repeat, HD), (1, 2, 0, 3))
    keys_g = jnp.transpose(keys_all.reshape(group_rows, local_kv, HD), (1, 0, 2))
    values_g = jnp.transpose(values_all.reshape(group_rows, local_kv, HD), (1, 0, 2))
    outs, lses = group_attention(query_g, keys_g, values_g, allowed, scale)
    attn = jnp.transpose(outs, (2, 0, 1, 3)).reshape(rows, local_heads * HD)
    attn_total = lax.psum(
        jnp.dot(attn, out_full, preferred_element_type=jnp.float32).astype(jnp.bfloat16), "tensor"
    ).astype(jnp.float32)
    resid1 = hidden_f + attn_total
    ffn_set = (
        lax.all_gather(ffn_gain, ("shard", "context"), axis=0, tiled=True),
        lax.all_gather(gate_weight, ("shard", "context"), axis=0, tiled=True),
        lax.all_gather(up_weight, ("shard", "context"), axis=0, tiled=True),
        lax.all_gather(down_weight, ("shard", "context"), axis=1, tiled=True),
    )
    gain_two, gate_full, up_full, down_full = ffn_set
    normed2, unit2, factor2 = norm_forward(resid1, gain_two)
    gate = jnp.dot(normed2, gate_full, preferred_element_type=jnp.float32)
    up_val = jnp.dot(normed2, up_full, preferred_element_type=jnp.float32)
    sigma = jax.nn.sigmoid(gate)
    silu_val = gate * sigma
    act = (silu_val * up_val).astype(jnp.bfloat16)
    ffn_total = lax.psum(
        jnp.dot(act, down_full, preferred_element_type=jnp.float32).astype(jnp.bfloat16), "tensor"
    ).astype(jnp.float32)
    block_out = (resid1 + ffn_total).astype(jnp.bfloat16)
    every_weight = (
        lax.all_gather(attn_gain, ("shard", "context"), axis=0, tiled=True),
        lax.all_gather(qkv_weight, ("shard", "context"), axis=0, tiled=True),
        lax.all_gather(qkv_bias, ("shard", "context"), axis=1, tiled=True),
        lax.all_gather(out_weight, ("shard", "context"), axis=1, tiled=True),
        lax.all_gather(ffn_gain, ("shard", "context"), axis=0, tiled=True),
        lax.all_gather(gate_weight, ("shard", "context"), axis=0, tiled=True),
        lax.all_gather(up_weight, ("shard", "context"), axis=0, tiled=True),
        lax.all_gather(down_weight, ("shard", "context"), axis=1, tiled=True),
    )
    gain_one, qkv_full, bias_full, out_full, gain_two, gate_full, up_full, down_full = every_weight
    d_act = contract_last(out_cotangent, down_full)
    d_gate = (d_act * up_val * sigma * (1.0 + gate * (1.0 - sigma))).astype(jnp.bfloat16)
    d_up = (d_act * silu_val).astype(jnp.bfloat16)
    grad_gate = contract_first(normed2, d_gate)
    grad_up = contract_first(normed2, d_up)
    grad_down = contract_first(act, out_cotangent)
    sum_gate, sum_up, sum_down = (
        lax.psum_scatter(grad_gate, ("shard", "context"), scatter_dimension=0, tiled=True),
        lax.psum_scatter(grad_up, ("shard", "context"), scatter_dimension=0, tiled=True),
        lax.psum_scatter(grad_down, ("shard", "context"), scatter_dimension=1, tiled=True),
    )
    d_normed2 = lax.psum(
        (contract_last(d_gate, gate_full) + contract_last(d_up, up_full)).astype(jnp.bfloat16),
        "tensor",
    ).astype(jnp.float32)
    grad_g2, d_back2 = norm_backward(d_normed2, unit2, factor2, gain_two)
    d_resid1 = out_cotangent.astype(jnp.float32) + d_back2
    d_resid1b = d_resid1.astype(jnp.bfloat16)
    grad_out = contract_first(attn, d_resid1b)
    d_attn = contract_last(d_resid1b, out_full).astype(jnp.bfloat16)
    d_attn_g = jnp.transpose(d_attn.reshape(rows, local_kv, repeat, HD), (1, 2, 0, 3))
    dquery, dkeys, dvalues = group_attention_back(
        query_g, keys_g, values_g, allowed, scale, outs, lses, d_attn_g
    )
    dkeys_rows = jnp.transpose(dkeys, (1, 0, 2)).reshape(group_rows, local_kv * HD)
    dvalues_rows = jnp.transpose(dvalues, (1, 0, 2)).reshape(group_rows, local_kv * HD)
    dkeys_mine, dvalues_mine = (
        lax.psum_scatter(
            dkeys_rows.astype(jnp.bfloat16), "context", scatter_dimension=0, tiled=True
        ).astype(jnp.float32),
        lax.psum_scatter(
            dvalues_rows.astype(jnp.bfloat16), "context", scatter_dimension=0, tiled=True
        ).astype(jnp.float32),
    )
    dquery = unrotate_pairs(
        jnp.transpose(dquery, (2, 0, 1, 3)).reshape(rows, local_heads, HD), cosine, sine
    )
    dkeys_mine = unrotate_pairs(dkeys_mine.reshape(rows, local_kv, HD), cosine, sine)
    d_proj = jnp.concatenate(
        [
            dquery.reshape(rows, local_heads * HD),
            dkeys_mine.reshape(rows, local_kv * HD),
            dvalues_mine,
        ],
        axis=1,
    )
    grad_bias = jnp.sum(d_proj, axis=0).reshape(local_heads + 2 * local_kv, HD)
    d_projb = d_proj.astype(jnp.bfloat16)
    grad_qkv = contract_first(normed1, d_projb)
    d_normed1 = lax.psum(contract_last(d_projb, qkv_full).astype(jnp.bfloat16), "tensor").astype(
        jnp.float32
    )
    grad_g1, d_back1 = norm_backward(d_normed1, unit1, factor1, gain_one)
    input_grad = d_resid1 + d_back1
    sum_g1, sum_qkv, sum_bias, sum_out, sum_g2 = (
        lax.psum_scatter(grad_g1, ("shard", "context"), scatter_dimension=0, tiled=True),
        lax.psum_scatter(grad_qkv, ("shard", "context"), scatter_dimension=0, tiled=True),
        lax.psum_scatter(grad_bias, ("shard", "context"), scatter_dimension=1, tiled=True),
        lax.psum_scatter(grad_out, ("shard", "context"), scatter_dimension=1, tiled=True),
        lax.psum_scatter(grad_g2, ("shard", "context"), scatter_dimension=0, tiled=True),
    )
    return (
        block_out,
        input_grad,
        sum_g1,
        sum_qkv,
        sum_bias,
        sum_out,
        sum_g2,
        sum_gate,
        sum_up,
        sum_down,
    )


def solution(mesh):
    placed = (
        P(("shard", "context"), None),
        P("shard", None),
        P(("shard", "context")),
        P(("shard", "context"), "tensor"),
        P("tensor", ("shard", "context")),
        P("tensor", ("shard", "context")),
        P(("shard", "context")),
        P(("shard", "context"), "tensor"),
        P(("shard", "context"), "tensor"),
        P("tensor", ("shard", "context")),
        P(("shard", "context"), None),
    )
    return jax.shard_map(
        local,
        mesh=mesh,
        in_specs=placed,
        out_specs=(
            P(("shard", "context"), None),
            P(("shard", "context"), None),
            P(("shard", "context")),
            P(("shard", "context"), "tensor"),
            P("tensor", ("shard", "context")),
            P("tensor", ("shard", "context")),
            P(("shard", "context")),
            P(("shard", "context"), "tensor"),
            P(("shard", "context"), "tensor"),
            P("tensor", ("shard", "context")),
        ),
        check_vma=False,
    )
```

profile of v0, /device:TPU:10, one launch (start us, length us, event | category | flops | bytes accessed | tf_op | source)
XLA Modules:
  0.0 1649.5 jit_solution(7359595490939998207)
XLA Ops:
  10.1 29.6 %all_gather.39 = bf16[8,128]{0,1:T(8,128)(2,1)S(1)} all-gather(bf16[8,8]{0,1:T(8,128)(2,1)S(1)} %copy.53), channel_id=1, replica_groups=mesh['shard'=4,'context'=4,'tensor'=2] {'shard','context'}, dimensions={1}, use_global_device_ids=true | all-gather | bytes 2176 | tf_op jit(solution)/shard_map/all_gather | solution.py:151
  39.7 1.4 fusion.84
  43.5 33.5 %all-reduce.6 = (bf16[1536]{0:T(1024)(128)(2,1)S(1)}, bf16[1536]{0:T(1024)(128)(2,1)S(1)}) all-reduce(bf16[1536]{0:T(1024)(128)(2,1)S(1)} %dynamic-update-slice, bf16[1536]{0:T(1024)(128)(2,1)S(1)} %dynamic-update-slice.1), channel_id=1, replica_groups=mesh['shard'=4,'context'=4,'tensor'=2] {'shard','context'}, use_global_device_ids=true, to_apply=%add | all-reduce | flops 3072 | bytes 12288
  80.6 2.6 convolution_add_fusion.1
  84.2 12.5 all_gather.40
  96.7 13.4 all_gather.41
  110.1 20.1 %while.48 = (s32[]{:T(128)}, bf16[6,128,128]{2,1,0:T(8,128)(2,1)}, f32[6,128]{1,0:T(8,128)}, bf16[6,128,128]{2,1,0:T(8,128)(2,1)S(1)}, bf16[512,128]{1,0:T(8,128...) while((s32[]{:T(128)}, bf16[6,128,128]{2,1,0:T(8,128)(2,1)}, ...), condition=%wide.region_5.6_spmd.clone, body=%wide.region_2.5_spmd.clone.sunk | while | flops 34226048 | bytes 1121921 | solution.py:94
  115.5 1.3 dynamic_update_slice.48
  118.9 1.3 dynamic_update_slice.48
  122.2 1.3 dynamic_update_slice.48
  132.0 3.4 convolution_convert_fusion.3
  137.4 24.8 %all-reduce.12.cloned.1.call-done = bf16[128,1536]{1,0:T(8,128)(2,1)} async-done(((bf16[128,1536]{1,0:T(8,128)(2,1)}), bf16[128,1536]{1,0:T(8,128)(2,1)}) %all-reduce.12.cloned.1.call-update) | async-done | bytes 393232 | tf_op jit(solution)/shard_map/psum | solution.py:178
  164.6 105.4 %all-gather.10.cloned.1.call-done = bf16[1536,4480]{1,0:T(8,128)(2,1)} async-done(((bf16[96,4480]{1,0:T(8,128)(2,1)}), bf16[1536,4480]{1,0:T(8,128)(2,1)}) %all-gather.10.cloned.1.call-update) | async-done | bytes 13762576 | tf_op jit(solution)/shard_map/all_gather | solution.py:184
  270.0 8.3 fusion.85
  278.3 99.7 %all-gather.12.cloned.1.call-done = bf16[1536,4480]{1,0:T(8,128)(2,1)} async-done(((bf16[96,4480]{1,0:T(8,128)(2,1)}), bf16[1536,4480]{1,0:T(8,128)(2,1)}) %all-gather.12.cloned.1.call-update) | async-done | bytes 13762576 | tf_op jit(solution)/shard_map/all_gather | solution.py:185
  378.0 8.3 fusion.86
  386.3 99.8 %all-gather.14.cloned.1.call-done = bf16[4480,1536]{0,1:T(8,128)(2,1)} async-done(((bf16[4480,96]{0,1:T(8,128)(2,1)}), bf16[4480,1536]{0,1:T(8,128)(2,1)}) %all-gather.14.cloned.1.call-update) | async-done | bytes 13762576 | tf_op jit(solution)/shard_map/all_gather | solution.py:186
  486.1 9.0 multiply_convert_fusion
  495.1 10.2 fusion.87
  505.3 10.2 fusion.33
  515.8 26.0 %all-reduce.14.cloned.1.call-done = bf16[128,1536]{1,0:T(8,128)(2,1)} async-done(((bf16[128,1536]{1,0:T(8,128)(2,1)}), bf16[128,1536]{1,0:T(8,128)(2,1)}) %all-reduce.14.cloned.1.call-update) | async-done | bytes 393232 | tf_op jit(solution)/shard_map/psum | solution.py:221
  541.8 2.0 fusion.47
  543.8 2.5 convolution_convert_fusion.4
  547.1 43.0 %while.49 = (s32[]{:T(128)}, f32[6,128,128]{1,2,0:T(8,128)}, f32[6,512,128]{2,1,0:T(8,128)}, f32[6,512,128]{2,1,0:T(8,128)}, bf16[6,128,128]{2,1,0:T(8,128)(2,1)...) while((s32[]{:T(128)}, f32[6,128,128]{1,2,0:T(8,128)}, ...), condition=%wide.region_13.14_spmd.clone, body=%wide.region_11.13_spmd.clone.sunk | while | flops 84688768 | bytes 2759333 | solution.py:105
  551.7 1.7 fusion.162
  558.9 1.7 fusion.162
  566.0 1.7 fusion.162
  573.2 1.7 fusion.162
  580.4 1.7 fusion.162
  587.6 1.7 fusion.162
  590.1 2.2 reduce_sum.115
  592.4 10.1 convolution_convert_fusion.2
  602.6 2.2 reduce_sum.114
  605.0 4.2 reduce-scatter.23.cloned.1.call-done
  610.0 19.6 %reduce-scatter.11.cloned.1.call-done = bf16[128,128]{1,0:T(8,128)(2,1)} async-done(((bf16[512,128]{1,0:T(8,128)(2,1)}), bf16[128,128]{1,0:T(8,128)(2,1)}) %reduce-scatter.11.cloned.1.call-update) | async-done | bytes 32784 | tf_op jit(solution)/shard_map/reduce_scatter | solution.py:237
  630.9 3.8 convolution_convert_fusion.1
  634.8 4.3 fusion.55
  639.8 3.7 fusion.58
  643.6 12.5 fusion.88
  656.1 12.3 fusion.89
  668.8 11.1 fusion.90
  681.5 1.4 fusion.50
  682.9 61.8 %all-reduce.5 = (f32[1536]{0:T(1024)S(1)}, f32[8,128]{1,0:T(8,128)S(1)}, f32[1536]{0:T(1024)S(1)}) all-reduce(f32[1536]{0:T(1024)S(1)} %get-tuple-element.310, f32[8,128]{1,0:T(8,128)S(1)} %bitcast.166, f32[1536]{0:T(1024)S(1)} %copy-done.13), channel_id=4, replica_groups=mesh['shard'=4,'context'=4,'tensor'=2] {'shard','context'}, use_global_device_ids=true, to_apply=%region_21.22.clone | all-reduce | flops 4096 | bytes 32768
  746.5 2.7 fusion.43
  750.5 88.5 %reduce-scatter.13.cloned.1.call-done = f32[96,1024]{1,0:T(8,128)} async-done(((f32[1536,1024]{1,0:T(8,128)}), f32[96,1024]{1,0:T(8,128)}) %reduce-scatter.13.cloned.1.call-update) | async-done | bytes 393232 | tf_op jit(solution)/shard_map/reduce_scatter | solution.py:266
  839.0 267.2 %reduce-scatter.17.cloned.1.call-done = f32[96,4480]{1,0:T(8,128)} async-done(((f32[1536,4480]{1,0:T(8,128)}), f32[96,4480]{1,0:T(8,128)}) %reduce-scatter.17.cloned.1.call-update) | async-done | bytes 1720336 | tf_op jit(solution)/shard_map/reduce_scatter | solution.py:217
  1106.1 268.4 %reduce-scatter.19.cloned.1.call-done = f32[96,4480]{1,0:T(8,128)} async-done(((f32[1536,4480]{1,0:T(8,128)}), f32[96,4480]{1,0:T(8,128)}) %reduce-scatter.19.cloned.1.call-update) | async-done | bytes 1720336 | tf_op jit(solution)/shard_map/reduce_scatter | solution.py:218
  1374.6 268.4 %reduce-scatter.21.cloned.1.call-done = f32[4480,96]{0,1:T(8,128)} async-done(((f32[4480,1536]{0,1:T(8,128)}), f32[4480,96]{0,1:T(8,128)}) %reduce-scatter.21.cloned.1.call-update) | async-done | bytes 1720336 | tf_op jit(solution)/shard_map/reduce_scatter | solution.py:219
  (219 shorter events, 72.1 us)
Async XLA Ops:
  7.2 73.4 %all-gather.6.cloned.1.call-start = ((), (), s32[]{:S(2)}) async-start(), calls=%async_computation.7 | async-start | bytes 3342336 | tf_op jit(solution)/shard_map/all_gather | solution.py:150
  7.9 124.1 %all-gather.8.cloned.1.call-start = ((), (), s32[]{:S(2)}) async-start(), calls=%async_computation.8 | async-start | bytes 2506752 | tf_op jit(solution)/shard_map/all_gather | solution.py:152
  8.7 153.6 %all-reduce.12.cloned.1.call-start = ((), (), s32[]{:S(2)}) async-start(), calls=%async_computation.9 | async-start | bytes 786432 | tf_op jit(solution)/shard_map/psum | solution.py:178
  8.8 75.0 %copy-start.18 = (f32[64]{0:T(128)}, f32[64]{0:T(128)S(1)}, u32[]{:S(2)}) copy-start(f32[64]{0:T(128)S(1)} %multiply_power_fusion) | copy-start | bytes 772
  78.2 5.1 copy-start.14
  80.3 3.5 copy-start.20
  80.5 3.0 copy-start.9
  80.6 3.0 copy-start.11
  130.2 0.7 copy-start.7
  132.0 4.6 copy-start.6
  132.0 30.2 %copy-start = (bf16[128,1536]{1,0:T(8,128)(2,1)S(1)}, bf16[128,1536]{1,0:T(8,128)(2,1)}, u32[]{:S(2)}) copy-start(bf16[128,1536]{1,0:T(8,128)(2,1)} %param.15) | copy-start | bytes 1179652
  135.4 134.6 %all-gather.10.cloned.1.call-start = ((), (), s32[]{:S(2)}) async-start(), calls=%async_computation.10 | async-start | bytes 14622720 | tf_op jit(solution)/shard_map/all_gather | solution.py:184
  136.0 242.0 %all-gather.12.cloned.1.call-start = ((), (), s32[]{:S(2)}) async-start(), calls=%async_computation.11 | async-start | bytes 14622720 | tf_op jit(solution)/shard_map/all_gather | solution.py:185
  136.6 349.5 %all-gather.14.cloned.1.call-start = ((), (), s32[]{:S(2)}) async-start(), calls=%async_computation.12 | async-start | bytes 14622720 | tf_op jit(solution)/shard_map/all_gather | solution.py:186
  137.2 404.6 %all-reduce.14.cloned.1.call-start = ((), (), s32[]{:S(2)}) async-start(), calls=%async_computation.13 | async-start | bytes 786432 | tf_op jit(solution)/shard_map/psum | solution.py:221
  163.5 380.3 %copy-start.16 = (f32[128]{0:T(128)}, f32[128]{0:T(128)S(1)}, u32[]{:S(2)}) copy-start(f32[128]{0:T(128)S(1)} %add_rsqrt_fusion) | copy-start | bytes 1540
  278.3 207.8 %copy-start.4 = (bf16[128,1536]{1,0:T(8,128)(2,1)S(1)}, bf16[128,1536]{1,0:T(8,128)(2,1)}, u32[]{:S(2)}) copy-start(bf16[128,1536]{1,0:T(8,128)(2,1)} %param.25) | copy-start | bytes 1179652
  495.1 10.2 copy-start.3
  495.1 10.2 copy-start.2
  505.3 36.5 %copy-start.1 = (bf16[128,1536]{1,0:T(8,128)(2,1)S(1)}, bf16[128,1536]{1,0:T(8,128)(2,1)}, u32[]{:S(2)}) copy-start(bf16[128,1536]{1,0:T(8,128)(2,1)} %all-reduce.12.cloned.1.call-done) | copy-start | bytes 1179652
  515.5 93.6 %reduce-scatter.23.cloned.1.call-start = ((), (), s32[]{:S(2)}) async-start(), calls=%async_computation.20 | async-start | bytes 163840
  543.8 3.3 copy-start.22
  592.3 37.3 %reduce-scatter.11.cloned.1.call-start = ((), (), s32[]{:S(2)}) async-start(), calls=%async_computation.14 | async-start | bytes 163840 | tf_op jit(solution)/shard_map/reduce_scatter | solution.py:237
  592.4 12.4 copy-start.8
  592.4 12.4 copy-start.10
  592.4 12.4 copy-start.12
  602.6 27.8 %copy-start.19 = (f32[64]{0:T(128)S(1)}, f32[64]{0:T(128)}, u32[]{:S(2)}) copy-start(f32[64]{0:T(128)} %copy-done.18) | copy-start | bytes 772
  602.6 27.8 %copy-start.21 = (f32[128]{0:T(128)S(1)}, f32[128]{0:T(128)}, u32[]{:S(2)}) copy-start(f32[128]{0:T(128)} %copy-done.20) | copy-start | bytes 1540
  604.8 76.7 %all-reduce.16.cloned.1.call-start = ((), (), s32[]{:S(2)}) async-start(), calls=%async_computation.21 | async-start | bytes 1572864 | tf_op jit(solution)/shard_map/psum | solution.py:195
  630.9 3.9 copy-start.17
  630.9 3.9 copy-start.23
  634.7 115.8 %reduce-scatter.15.cloned.1.call-start = ((), (), s32[]{:S(2)}) async-start(), calls=%async_computation.16 | async-start | bytes 5013504 | tf_op jit(solution)/shard_map/reduce_scatter | solution.py:268
  639.1 0.7 copy-start.15
  639.1 199.8 %reduce-scatter.13.cloned.1.call-start = ((), (), s32[]{:S(2)}) async-start(), calls=%async_computation.15 | async-start | bytes 6684672 | tf_op jit(solution)/shard_map/reduce_scatter | solution.py:266
  643.5 462.6 %reduce-scatter.17.cloned.1.call-start = ((), (), s32[]{:S(2)}) async-start(), calls=%async_computation.17 | async-start | bytes 29245440 | tf_op jit(solution)/shard_map/reduce_scatter | solution.py:217
  656.0 718.5 %reduce-scatter.19.cloned.1.call-start = ((), (), s32[]{:S(2)}) async-start(), calls=%async_computation.18 | async-start | bytes 29245440 | tf_op jit(solution)/shard_map/reduce_scatter | solution.py:218
  668.5 974.5 %reduce-scatter.21.cloned.1.call-start = ((), (), s32[]{:S(2)}) async-start(), calls=%async_computation.19 | async-start | bytes 29245440 | tf_op jit(solution)/shard_map/reduce_scatter | solution.py:219
  679.9 3.0 copy-start.13
  679.9 66.6 %copy-start.5 = (bf16[128,1536]{1,0:T(8,128)(2,1)S(1)}, bf16[128,1536]{1,0:T(8,128)(2,1)}, u32[]{:S(2)}) copy-start(bf16[128,1536]{1,0:T(8,128)(2,1)} %all-reduce.14.cloned.1.call-done) | copy-start | bytes 1179652
Sparse Core Ops, SparseCore 0:
  10.3 46.1 all-gather.5
  58.8 40.5 all-gather.7
  135.5 26.6 all-reduce.11
  164.4 105.5 all-gather.9
  272.1 105.8 all-gather.11
  380.2 105.8 all-gather.13
  515.7 26.0 all-reduce.13
  592.5 16.6 reduce-scatter.22
  612.0 17.5 reduce-scatter.10
  634.9 35.3 all-reduce.15
  674.7 75.7 reduce-scatter.14
  754.9 84.0 reduce-scatter.12
  843.6 262.4 reduce-scatter.16
  1110.7 263.8 reduce-scatter.18
  1379.1 263.8 reduce-scatter.20
where the time goes:
time: 1660 us; the launch traced here: 1650 us
  waiting for transfers between devices  1280 us (77%)
  blocking collectives  151 us (9%)
  matrix products  147 us (9%)
  local copies, waits for them, and re-layouts  33.1 us (2%)
  other arithmetic  24.1 us (1%)
    reduce_scatter x1, waiting for transfers between devices, local(): lax.psum_scatter(grad_up, ('shard', 'context'), scatter_dimension=0, tile...  268 us
    reduce_scatter x1, waiting for transfers between devices, local(): lax.psum_scatter(grad_down, ('shard', 'context'), scatter_dimension=1, ti...  268 us
    reduce_scatter x1, waiting for transfers between devices, local(): lax.psum_scatter(grad_gate, ('shard', 'context'), scatter_dimension=0, ti...  267 us
    all_gather x1, waiting for transfers between devices, local(): lax.all_gather(gate_weight, ('shard', 'context'), axis=0, tiled=True)  105 us
    all_gather x1, waiting for transfers between devices, local(): lax.all_gather(down_weight, ('shard', 'context'), axis=1, tiled=True)  99.8 us
    all_gather x1, waiting for transfers between devices, local(): lax.all_gather(up_weight, ('shard', 'context'), axis=0, tiled=True)  99.7 us
    unnamed x2, blocking collectives  95.3 us
    reduce_scatter x1, waiting for transfers between devices, local(): lax.psum_scatter(grad_qkv, ('shard', 'context'), scatter_dimension=0, til...  88.5 us
  transfers between devices with their start and end apart: 15, of which 12 were waited for; matrix products, arithmetic and copies ran while one was open for 7% of the time, Pallas kernels for 0%

commit v1 on v0

v1 whole, which is shorter than its diff:
```python
import functools

import jax
import jax.numpy as jnp
from jax import lax
from jax.experimental import pallas as pl
from jax.experimental.pallas import tpu as pltpu
from jax.sharding import PartitionSpec as P

H = 12
KVH = 2
HD = 128
LANES = 128
SUBLANES = 16
BF16 = jnp.bfloat16
F32 = jnp.float32

EPSILON = 1e-06
THETA = 1000000.0

OWNERS = ("shard", "context")
TEAM = ("context", "tensor")
MESH = pl.DeviceIdType.MESH
VMEM_BYTES = 62 * 1024 * 1024


def dot(left, right):
    return jnp.dot(left, right, preferred_element_type=F32)


def contract_last(left, right):
    return lax.dot_general(left, right, (((1,), (1,)), ((), ())), preferred_element_type=F32)


def contract_first(left, right):
    return lax.dot_general(left, right, (((0,), (0,)), ((), ())), preferred_element_type=F32)


def batched(left, right, left_dim, right_dim):
    return lax.dot_general(
        left, right, (((left_dim,), (right_dim,)), ((0,), (0,))), preferred_element_type=F32
    )


def norm_forward(values, gain):
    factor = lax.rsqrt(jnp.mean(values * values, axis=1, keepdims=True) + EPSILON)
    unit = values * factor
    return ((unit * gain).astype(BF16), unit, factor)


def norm_backward(grad_out, unit, factor, gain):
    gain_grad = jnp.sum(grad_out * unit, axis=0)
    scaled = grad_out * gain
    return (gain_grad, factor * (scaled - unit * jnp.mean(scaled * unit, axis=1, keepdims=True)))


def rotary_tables(positions):
    half = HD // 2
    freqs = THETA ** (-(2.0 * jnp.arange(half, dtype=F32)) / HD)
    angles = positions.astype(F32)[:, None] * freqs[None, :]
    cosine, sine = jnp.cos(angles), jnp.sin(angles)
    return (
        jnp.concatenate([cosine, cosine], axis=1),
        jnp.concatenate([-sine, sine], axis=1),
    )


def swap_halves(values):
    half = values.shape[-1] // 2
    return jnp.concatenate([values[..., half:], values[..., :half]], axis=-1)


def rotate(values, cosine, sine):
    return values * cosine + swap_halves(values) * sine


def unrotate(values, cosine, sine):
    return values * cosine - swap_halves(values) * sine


class Place:
    def __init__(self, ns, nz):
        self.ns, self.nz, self.no = ns, nz, ns // 2
        self.s, self.z, self.y = (lax.axis_index(a) for a in ("shard", "context", "tensor"))
        self.core = lax.rem(self.s, 2)
        self.outer = lax.div(self.s, 2)
        self.mate = self.s + 1 - 2 * self.core
        self.twin = 1 - self.y

    def z_to(self, d):
        return lax.rem(self.z + d, self.nz)

    def z_from(self, d):
        return lax.rem(self.z - d + self.nz, self.nz)

    def s_to(self, o):
        return lax.rem(self.outer + o, self.no) * 2 + self.core

    def s_from(self, o):
        return lax.rem(self.outer - o + self.no, self.no) * 2 + self.core

    def mate_from(self, o):
        return lax.rem(self.outer - o + self.no, self.no) * 2 + 1 - self.core

    def greet(self):
        barrier = pltpu.get_barrier_semaphore()
        peers = [{"context": self.z_to(d)} for d in range(1, self.nz)]
        peers += [{"shard": self.s_to(o)} for o in range(1, self.no)]
        peers += [{"shard": self.mate}, {"tensor": self.twin}]
        for peer in peers:
            pl.semaphore_signal(barrier, inc=1, device_id=peer, device_id_type=MESH)
        pl.semaphore_wait(barrier, len(peers))


class Sends:
    def __init__(self):
        self.remote, self.local = [], []

    def go(self, src, dst, send, recv, **peer):
        copy = pltpu.make_async_remote_copy(
            src_ref=src, dst_ref=dst, send_sem=send, recv_sem=recv,
            device_id=peer, device_id_type=MESH,
        )
        copy.start()
        self.remote.append(copy)

    def here(self, src, dst, sem):
        copy = pltpu.make_async_copy(src, dst, sem)
        copy.start()
        self.local.append(copy)

    def drain(self):
        for copy in self.remote:
            copy.wait_send()
        for copy in self.local:
            copy.wait()
        self.remote, self.local = [], []


def landed(ref, send, recv, **peer):
    pltpu.make_async_remote_copy(
        src_ref=ref, dst_ref=ref, send_sem=send, recv_sem=recv,
        device_id=peer, device_id_type=MESH,
    ).wait_recv()


class Spread:
    def __init__(self, at, sends, src, dst, sems):
        self.at, self.sends, self.src, self.dst = at, sends, src, dst
        self.copy = None
        self.own, self.zs, self.zr, self.xs, self.xr, self.cs, self.cr = sems

    @staticmethod
    def sems(ns, nz):
        dma, no = pltpu.SemaphoreType.DMA, ns // 2
        return [
            dma, dma((nz,)), dma((nz,)), dma((nz, no)), dma((nz, no)), dma((no, nz)), dma((no, nz)),
        ]

    def over_z(self):
        at = self.at
        for d in range(1, at.nz):
            z2 = at.z_to(d)
            self.sends.go(self.src(z2), self.dst(at.s, at.z), self.zs.at[d], self.zr.at[d], context=z2)

    def over_s(self, d, ref):
        at = self.at
        for o in range(1, at.no):
            self.sends.go(
                ref, self.dst(at.s, at.z_from(d)), self.xs.at[d, o], self.xr.at[d, o],
                shard=at.s_to(o),
            )
        self.sends.go(
            ref, self.dst(at.s, at.z_from(d)), self.cs.at[0, d], self.cr.at[0, d], shard=at.mate
        )

    def own_block(self):
        at = self.at
        self.over_s(0, self.src(at.z))
        self.copy = pltpu.make_async_copy(self.src(at.z), self.dst(at.s, at.z), self.own)
        self.copy.start()

    def pass_z(self, d):
        at = self.at
        ref = self.dst(at.s, at.z_from(d))
        landed(ref, self.zs.at[d], self.zr.at[d], context=at.z_from(d))
        self.over_s(d, ref)

    def pass_s(self, o, d):
        at = self.at
        s1 = at.s_from(o)
        ref = self.dst(s1, at.z_from(d))
        landed(ref, self.xs.at[d, o], self.xr.at[d, o], shard=s1)
        self.sends.go(ref, ref, self.cs.at[o, d], self.cr.at[o, d], shard=at.mate)

    def finish(self):
        at = self.at
        self.copy.wait()
        for o in range(at.no):
            for d in range(at.nz):
                ref = self.dst(at.mate_from(o), at.z_from(d))
                landed(ref, self.cs.at[o, d], self.cr.at[o, d], shard=at.mate)

    def pass_all(self):
        for d in range(1, self.at.nz):
            self.pass_z(d)
        for o in range(1, self.at.no):
            for d in range(self.at.nz):
                self.pass_s(o, d)


class Tokens:
    def __init__(self, at, sends, ref, sems):
        self.at, self.sends, self.ref = at, sends, ref
        self.zs, self.zr, self.ys, self.yr = sems

    @staticmethod
    def sems(nz):
        dma = pltpu.SemaphoreType.DMA
        return [dma((nz,)), dma((nz,)), dma((nz,)), dma((nz,))]

    def over_z(self, src):
        at = self.at
        for d in range(1, at.nz):
            self.sends.go(
                src, self.ref.at[at.z, at.y], self.zs.at[d], self.zr.at[d], context=at.z_to(d)
            )

    def over_y(self, d, src):
        at = self.at
        self.sends.go(
            src, self.ref.at[at.z_from(d), at.y], self.ys.at[d], self.yr.at[d], tensor=at.twin
        )

    def pass_z(self, d):
        at = self.at
        ref = self.ref.at[at.z_from(d), at.y]
        landed(ref, self.zs.at[d], self.zr.at[d], context=at.z_from(d))
        self.over_y(d, ref)

    def wait_y(self, d):
        at = self.at
        ref = self.ref.at[at.z_from(d), at.twin]
        landed(ref, self.ys.at[d], self.yr.at[d], tensor=at.twin)


def whole_lines(small, blocks, depth):
    tiles = []
    for t in range(blocks * depth // LANES):
        tile = jnp.zeros((8, LANES), F32)
        lane = lax.broadcasted_iota(jnp.int32, (8, LANES), 1) + t * LANES
        for b in range(t * LANES // depth, min(blocks, -(-(t + 1) * LANES // depth))):
            line = small[b, :8, :].astype(F32)
            shift = (b * depth - t * LANES) % LANES
            moved = pltpu.roll(line, shift, 1) if shift else line
            tile = jnp.where((lane >= b * depth) & (lane < (b + 1) * depth), moved, tile)
        tiles.append(tile)
    return jnp.concatenate(tiles, axis=1)


def front_kernel(ns, nz, heads, kv, *refs):
    ins, outs, (small, ypart, yland, *sems) = refs[:10], refs[10:22], refs[22:]
    (wa_in, small_in, gate_in, up_in, down_in, hidden, cot_in, cosine, sine, mask) = ins
    (wa, gate_w, up_w, down_w, lines, n2, cot, resid, query, kv_all, probs, attn) = outs
    n_spread = len(Spread.sems(ns, nz))
    n_tokens = len(Tokens.sems(nz))
    at, sends = Place(ns, nz), Sends()
    depth = wa_in.shape[0]
    rows, width = hidden.shape
    half = rows // 2
    q_cols = heads * HD
    qkv_cols = q_cols + 2 * kv * HD

    def spread(i, src, dst):
        return Spread(at, sends, src, dst, sems[i * n_spread:(i + 1) * n_spread])

    def block(ref):
        return lambda s1, z1: ref.at[pl.ds(pl.multiple_of((s1 * nz + z1) * depth, SUBLANES), depth)]

    w_attn = spread(0, lambda z2: wa_in, block(wa))
    w_small = spread(1, lambda z2: small_in, lambda s1, z1: small.at[s1 * nz + z1])
    ffn = [
        spread(2 + i, lambda z2, src=src: src.at[z2], block(dst))
        for i, (src, dst) in enumerate(((gate_in, gate_w), (up_in, up_w), (down_in, down_w)))
    ]
    rest = sems[5 * n_spread:]
    t_cot = Tokens(at, sends, cot, rest[:n_tokens])
    t_n2 = Tokens(at, sends, n2, rest[n_tokens:2 * n_tokens])
    kvs, kvr, yps, ypr, cot_sem = rest[2 * n_tokens:]

    at.greet()
    w_small.over_z()
    w_small.own_block()
    w_attn.over_z()
    w_attn.own_block()
    ffn[0].over_z()
    ffn[0].own_block()
    my_half = cot_in.at[pl.ds(pl.multiple_of(at.y * half, SUBLANES), half)]
    sends.here(cot_in.at[pl.ds(0, half)], cot.at[at.z, 0], cot_sem.at[0])
    sends.here(cot_in.at[pl.ds(half, half)], cot.at[at.z, 1], cot_sem.at[1])

    hidden_f = hidden[...].astype(F32)
    factor1 = lax.rsqrt(jnp.mean(hidden_f * hidden_f, axis=1, keepdims=True) + EPSILON)
    w_small.pass_all()
    w_attn.pass_all()
    w_small.finish()
    gains = whole_lines(small, ns * nz, depth)
    lines[...] = gains
    normed1 = (hidden[...].astype(F32) * factor1 * gains[0:1, :]).astype(BF16)
    w_attn.finish()

    width_each = HD // (ns * nz)
    lane = lax.broadcasted_iota(jnp.int32, (8, LANES), 1)
    bias = jnp.zeros((8, LANES), F32)
    for b in range(ns * nz):
        line = small[b, 8:16, :].astype(F32)
        moved = pltpu.roll(line, b * width_each, 1) if b else line
        bias = jnp.where((lane >= b * width_each) & (lane < (b + 1) * width_each), moved, bias)
    cos_t, sin_t = cosine[...], sine[...]

    def projected(head):
        part = jnp.dot(
            normed1, wa[:, head * HD:(head + 1) * HD], preferred_element_type=F32
        )
        return part + bias[head:head + 1, :]

    def rotated(values):
        return values * cos_t + pltpu.roll(values, HD // 2, 1) * sin_t

    for j in range(kv):
        kv_all[at.z, :, j * HD:(j + 1) * HD] = rotated(projected(heads + j)).astype(BF16)
        kv_all[at.z, :, (kv + j) * HD:(kv + j + 1) * HD] = projected(heads + kv + j).astype(BF16)
    for d in range(1, nz):
        sends.go(kv_all.at[at.z], kv_all.at[at.z], kvs.at[d], kvr.at[d], context=at.z_to(d))
    ffn[1].over_z()
    ffn[1].own_block()
    t_cot.over_z(my_half)
    ffn[0].pass_all()
    for h in range(heads):
        query[:, h * HD:(h + 1) * HD] = rotated(projected(h)).astype(BF16)
    for d in range(1, nz):
        src = kv_all.at[at.z_from(d)]
        landed(src, kvs.at[d], kvr.at[d], context=at.z_from(d))

    scale = HD ** (-0.5)
    group_rows = nz * rows
    keep = mask[...] > 0
    repeat = heads // kv
    for h in range(heads):
        j = h // repeat
        keys = kv_all[:, :, j * HD:(j + 1) * HD].reshape(group_rows, HD)
        values = kv_all[:, :, (kv + j) * HD:(kv + j + 1) * HD].reshape(group_rows, HD)
        scores = lax.dot_general(
            query[:, h * HD:(h + 1) * HD], keys, (((1,), (1,)), ((), ())),
            preferred_element_type=F32,
        )
        scores = jnp.where(keep, scores * scale, -1e30)
        peak = jnp.max(scores, axis=1, keepdims=True)
        lse = peak + jnp.log(jnp.sum(jnp.exp(scores - peak), axis=1, keepdims=True))
        p = jnp.exp(scores - lse)
        probs[h * rows:(h + 1) * rows, :] = p
        out = jnp.dot(p.astype(BF16), values, preferred_element_type=F32)
        attn[:, h * HD:(h + 1) * HD] = out.astype(BF16)
    part = lax.dot_general(
        attn[...], wa[:, qkv_cols:qkv_cols + q_cols], (((1,), (1,)), ((), ())),
        preferred_element_type=F32,
    ).astype(BF16)
    ypart[0] = part[:half]
    ypart[1] = part[half:]
    sends.go(ypart.at[at.twin], yland, yps, ypr, tensor=at.twin)
    ffn[2].over_z()
    ffn[2].own_block()
    for d in range(1, nz):
        t_cot.pass_z(d)
    ffn[1].pass_all()

    landed(yland, yps, ypr, tensor=at.twin)
    base = pl.multiple_of(at.y * half, SUBLANES)
    total = ypart[at.y].astype(F32) + yland[...].astype(F32)
    res = hidden[pl.ds(base, half), :].astype(F32) + total
    resid[...] = res
    factor2 = lax.rsqrt(jnp.mean(res * res, axis=1, keepdims=True) + EPSILON)
    n2[at.z, at.y] = (res * factor2 * gains[1:2, :]).astype(BF16)
    t_n2.over_z(n2.at[at.z, at.y])
    t_n2.over_y(0, n2.at[at.z, at.y])
    for d in range(1, nz):
        t_n2.pass_z(d)
    ffn[2].pass_all()
    for d in range(nz):
        t_n2.wait_y(d)
    for d in range(1, nz):
        t_cot.wait_y(d)
    for item in ffn:
        item.finish()
    sends.drain()


def front(ns, nz, heads, kv, wa_in, small_in, ffn_in, hidden, cot, cosine, sine, mask):
    rows, width = hidden.shape
    owners = ns * nz
    half = rows // 2
    unit = ffn_in[0].shape[2]
    wide = owners * wa_in.shape[0]
    dma = pltpu.SemaphoreType.DMA
    shape = jax.ShapeDtypeStruct
    vmem = pl.BlockSpec(memory_space=pltpu.VMEM)
    anyspace = pl.BlockSpec(memory_space=pl.ANY)
    return pl.pallas_call(
        functools.partial(front_kernel, ns, nz, heads, kv),
        out_shape=[
            shape((wide, wa_in.shape[1]), BF16),
            *[shape((wide, unit), BF16)] * 3,
            shape((8, wide), F32),
            shape((nz, 2, half, width), BF16),
            shape((nz, 2, half, width), BF16),
            shape((half, width), F32),
            shape((rows, heads * HD), BF16),
            shape((nz, rows, 2 * kv * HD), BF16),
            shape((heads * rows, nz * rows), F32),
            shape((rows, heads * HD), BF16),
        ],
        in_specs=[anyspace] * 5 + [vmem, anyspace] + [vmem] * 3,
        out_specs=[vmem] + [anyspace] * 3 + [vmem] * 8,
        scratch_shapes=[
            pltpu.VMEM((owners, 16, LANES), BF16),
            pltpu.VMEM((2, half, width), BF16),
            pltpu.VMEM((half, width), BF16),
        ]
        + Spread.sems(ns, nz) * 5
        + Tokens.sems(nz) * 2
        + [dma((nz,)), dma((nz,)), dma, dma, dma((2,))],
        compiler_params=pltpu.CompilerParams(
            collective_id=0, has_side_effects=True, vmem_limit_bytes=VMEM_BYTES
        ),
    )(wa_in, small_in, *ffn_in, hidden, cot, cosine, sine, mask)


def fast_step(
    ns,
    nz,
    hidden_in,
    segment_ids,
    attn_gain,
    qkv_weight,
    qkv_bias,
    out_weight,
    ffn_gain,
    gate_weight,
    up_weight,
    down_weight,
    out_cotangent,
):
    rows, width = hidden_in.shape
    depth, hidden_units = gate_weight.shape
    parts = 2
    heads = H // parts
    kv = KVH // parts
    repeat = heads // kv
    scale = HD ** (-0.5)
    block_index = lax.axis_index("context")
    part_index = lax.axis_index("tensor")
    half_rows = rows // parts
    unit_cols = -(-hidden_units // (nz * LANES)) * LANES
    padded = unit_cols * nz
    q_cols = heads * HD
    k_cols = kv * HD

    def by_place(weight):
        full = jnp.pad(weight, ((0, 0), (0, padded - hidden_units)))
        return jnp.transpose(full.reshape(depth, nz, unit_cols), (1, 0, 2))

    ffn_in = [by_place(w) for w in (gate_weight, up_weight, down_weight.T)]
    wa_in = jnp.concatenate([qkv_weight, out_weight.T], axis=1)
    gains_in = jnp.pad(jnp.stack([attn_gain, ffn_gain]), ((0, 6), (0, LANES - depth)))
    bias_in = jnp.pad(qkv_bias, ((0, 0), (0, LANES - qkv_bias.shape[1])))
    small_in = jnp.concatenate([gains_in, bias_in], axis=0)

    seg_all = segment_ids[0]
    group_rows = seg_all.shape[0]
    first_row = block_index * rows
    index_all = jnp.arange(group_rows, dtype=jnp.int32)
    seg_local = lax.dynamic_slice_in_dim(seg_all, first_row, rows)
    index_local = first_row + jnp.arange(rows, dtype=jnp.int32)
    earlier = jnp.sum((seg_all[None, :] < seg_local[:, None]).astype(jnp.int32), axis=1)
    allowed = (seg_local[:, None] == seg_all[None, :]) & (
        index_local[:, None] >= index_all[None, :]
    )
    cosine, sine = rotary_tables(index_local - earlier)

    wa, gate_full, up_full, down_full, lines, n2, cot, resid_half, query, kv_all, p_soft, attn = front(
        ns, nz, heads, kv, wa_in, small_in, ffn_in, hidden_in, out_cotangent, cosine, sine,
        allowed.astype(F32),
    )
    gain_one, gain_two = lines[0], lines[1]
    qkv_full = wa[:, : q_cols + 2 * k_cols]
    out_full = wa[:, q_cols + 2 * k_cols :]
    normed2 = n2.reshape(group_rows, width)
    cot = cot.reshape(group_rows, width)
    hidden_f = hidden_in.astype(F32)
    normed1, unit1, factor1 = norm_forward(hidden_f, gain_one)
    _, unit2, factor2 = norm_forward(resid_half, gain_two)
    query = jnp.transpose(query.reshape(rows, heads, HD), (1, 0, 2)).reshape(kv, repeat * rows, HD)
    kv_rows = kv_all.reshape(group_rows, 2 * kv, HD)
    keys = jnp.transpose(kv_rows[:, :kv], (1, 0, 2))
    values = jnp.transpose(kv_rows[:, kv:], (1, 0, 2))
    p_soft = p_soft.reshape(kv, repeat * rows, group_rows)
    probs = p_soft.astype(BF16)
    outs = jnp.transpose(attn.reshape(rows, heads, HD), (1, 0, 2)).reshape(kv, repeat * rows, HD)
    mine = part_index * half_rows
    cot_half = lax.dynamic_slice_in_dim(out_cotangent, mine, half_rows)
    blocks = nz
    gate = dot(normed2, gate_full)
    up_val = dot(normed2, up_full)
    sigma = jax.nn.sigmoid(gate)
    silu_val = gate * sigma
    act = (silu_val * up_val).astype(BF16)
    ffn_part = contract_last(act, down_full).astype(BF16)
    d_act = dot(cot, down_full)
    d_gate = (d_act * up_val * sigma * (1.0 + gate * (1.0 - sigma))).astype(BF16)
    d_up = (d_act * silu_val).astype(BF16)
    dn2_part = (contract_last(d_gate, gate_full) + contract_last(d_up, up_full)).astype(BF16)
    ffn_half = lax.psum_scatter(ffn_part, TEAM, scatter_dimension=0, tiled=True)
    block_half = (resid_half + ffn_half.astype(F32)).astype(BF16)
    block_out = lax.all_gather(block_half, "tensor", axis=0, tiled=True)
    dn2_half = lax.psum_scatter(dn2_part, TEAM, scatter_dimension=0, tiled=True).astype(F32)
    grad_g2, d_back2 = norm_backward(dn2_half, unit2, factor2, gain_two)
    d_resid_half = cot_half.astype(F32) + d_back2

    def give_back(grad):
        part = lax.psum_scatter(grad.astype(BF16), "shard", scatter_dimension=0, tiled=True)
        part = part.reshape(blocks, depth, unit_cols)
        part = lax.all_to_all(part, "context", split_axis=0, concat_axis=2, tiled=True)
        return part.reshape(depth, padded)[:, :hidden_units].astype(F32)

    sum_gate = give_back(contract_first(normed2, d_gate))
    sum_up = give_back(contract_first(normed2, d_up))
    sum_down = give_back(contract_first(cot, act)).T

    d_resid_b = lax.all_gather(d_resid_half.astype(BF16), "tensor", axis=0, tiled=True)
    grad_out = contract_first(d_resid_b, attn)
    d_attn = dot(d_resid_b, out_full).astype(BF16)
    d_outs = jnp.transpose(d_attn.reshape(rows, heads, HD), (1, 0, 2)).reshape(
        kv, repeat * rows, HD
    )
    d_prob = batched(d_outs, values, 2, 2)
    delta = jnp.sum(d_outs.astype(F32) * outs.astype(F32), axis=2, keepdims=True)
    d_score = (p_soft * (d_prob - delta)).astype(BF16)
    d_query = batched(d_score, keys, 2, 1) * scale
    d_keys = batched(d_score, query, 1, 1) * scale
    d_values = batched(probs, d_outs, 1, 1)
    d_kv = jnp.concatenate([d_keys, d_values], axis=0).astype(BF16)
    d_kv = lax.psum_scatter(d_kv, "context", scatter_dimension=1, tiled=True).astype(F32)
    d_query = unrotate(d_query.reshape(heads, rows, HD), cosine, sine)
    d_keys = unrotate(d_kv[:kv], cosine, sine)
    d_proj = jnp.transpose(jnp.concatenate([d_query, d_keys, d_kv[kv:]], axis=0), (1, 0, 2))
    grad_bias = jnp.sum(d_proj, axis=0)
    d_projb = d_proj.reshape(rows, -1).astype(BF16)
    grad_qkv = contract_first(normed1, d_projb)
    dn1_part = contract_last(d_projb, qkv_full).astype(BF16)
    dn1_half = lax.psum_scatter(dn1_part, "tensor", scatter_dimension=0, tiled=True).astype(F32)
    unit1_half = lax.dynamic_slice_in_dim(unit1, mine, half_rows)
    factor1_half = lax.dynamic_slice_in_dim(factor1, mine, half_rows)
    grad_g1, d_back1 = norm_backward(dn1_half, unit1_half, factor1_half, gain_one)
    input_grad = lax.all_gather(d_resid_half + d_back1, "tensor", axis=0, tiled=True)

    gains = lax.psum(jnp.stack([grad_g1, grad_g2]), "tensor")
    sum_gains = lax.psum_scatter(gains, OWNERS, scatter_dimension=1, tiled=True)
    sum_qkv = lax.psum_scatter(grad_qkv.astype(BF16), OWNERS, scatter_dimension=0, tiled=True)
    sum_bias = lax.psum_scatter(grad_bias, OWNERS, scatter_dimension=1, tiled=True)
    sum_out = lax.psum_scatter(grad_out.astype(BF16), OWNERS, scatter_dimension=0, tiled=True)
    return (
        block_out,
        input_grad,
        sum_gains[0],
        sum_qkv.astype(F32),
        sum_bias,
        sum_out.astype(F32).T,
        sum_gains[1],
        sum_gate,
        sum_up,
        sum_down,
    )


def general_step(
    hidden_in,
    segment_ids,
    attn_gain,
    qkv_weight,
    qkv_bias,
    out_weight,
    ffn_gain,
    gate_weight,
    up_weight,
    down_weight,
    out_cotangent,
):
    rows, width = hidden_in.shape
    depth = gate_weight.shape[0]
    hidden_units = gate_weight.shape[1]
    parts = lax.axis_size("tensor")
    blocks = lax.axis_size("context")
    heads = H // parts
    kv = KVH // parts
    repeat = H // KVH
    scale = HD ** (-0.5)
    block_index = lax.axis_index("context")
    part_index = lax.axis_index("tensor")
    half_rows = rows // parts
    unit_cols = -(-hidden_units // (blocks * LANES)) * LANES
    padded = unit_cols * blocks

    def spread(weight):
        full = jnp.pad(weight, ((0, 0), (0, padded - hidden_units)))
        mine = lax.all_to_all(full, "context", split_axis=1, concat_axis=0, tiled=True)
        mine = mine.reshape(blocks * depth, unit_cols)
        return lax.all_gather(mine, "shard", axis=0, tiled=True)

    gate_full = spread(gate_weight)
    up_full = spread(up_weight)
    down_full = spread(down_weight.T)
    gain_one = lax.all_gather(attn_gain, OWNERS, axis=0, tiled=True).astype(F32)
    gain_two = lax.all_gather(ffn_gain, OWNERS, axis=0, tiled=True).astype(F32)
    bias = lax.all_gather(qkv_bias, OWNERS, axis=1, tiled=True).reshape(-1).astype(F32)
    qkv_full = lax.all_gather(qkv_weight, OWNERS, axis=0, tiled=True)
    out_full = lax.all_gather(out_weight.T, OWNERS, axis=0, tiled=True)

    seg_all = segment_ids[0]
    group_rows = seg_all.shape[0]
    first_row = block_index * rows
    index_all = jnp.arange(group_rows, dtype=jnp.int32)
    earlier = jnp.sum((seg_all[None, :] < seg_all[:, None]).astype(jnp.int32), axis=1)
    positions = index_all - earlier
    seg_local = lax.dynamic_slice_in_dim(seg_all, first_row, rows)
    index_local = first_row + jnp.arange(rows, dtype=jnp.int32)
    allowed = (seg_local[:, None] == seg_all[None, :]) & (
        index_local[:, None] >= index_all[None, :]
    )
    cosine, sine = rotary_tables(positions)
    cos_local = lax.dynamic_slice_in_dim(cosine, first_row, rows)
    sin_local = lax.dynamic_slice_in_dim(sine, first_row, rows)

    hidden_all = lax.all_gather(hidden_in, "context", axis=0, tiled=True)
    normed_all, _, _ = norm_forward(hidden_all.astype(F32), gain_one)
    hidden_f = hidden_in.astype(F32)
    normed1, unit1, factor1 = norm_forward(hidden_f, gain_one)
    q_cols = heads * HD
    k_cols = kv * HD
    query_f = dot(normed1, qkv_full[:, :q_cols]) + bias[:q_cols]
    kv_f = dot(normed_all, qkv_full[:, q_cols:]) + bias[q_cols:]
    query = jnp.transpose(query_f.reshape(rows, heads, HD), (1, 0, 2))
    query = rotate(query, cos_local, sin_local).astype(BF16)
    keys = jnp.transpose(kv_f[:, :k_cols].reshape(group_rows, kv, HD), (1, 0, 2))
    keys = rotate(keys, cosine, sine).astype(BF16)
    values = jnp.transpose(kv_f[:, k_cols:].reshape(group_rows, kv, HD), (1, 0, 2)).astype(BF16)
    query = query.reshape(kv, repeat * rows, HD)
    mask = jnp.tile(allowed, (repeat, 1))
    scores = jnp.where(mask, batched(query, keys, 2, 2) * scale, -1e30)
    peak = jnp.max(scores, axis=2, keepdims=True)
    lse = peak + jnp.log(jnp.sum(jnp.exp(scores - peak), axis=2, keepdims=True))
    p_soft = jnp.exp(scores - lse)
    probs = p_soft.astype(BF16)
    outs = batched(probs, values, 2, 1).astype(BF16)
    attn = jnp.transpose(outs.reshape(heads, rows, HD), (1, 0, 2)).reshape(rows, q_cols)
    attn_part = contract_last(attn, out_full).astype(BF16)

    mine = part_index * half_rows
    attn_half = lax.psum_scatter(attn_part, "tensor", scatter_dimension=0, tiled=True)
    resid_half = lax.dynamic_slice_in_dim(hidden_f, mine, half_rows) + attn_half.astype(F32)
    normed2_half, unit2, factor2 = norm_forward(resid_half, gain_two)
    normed2 = lax.all_gather(normed2_half, TEAM, axis=0, tiled=True)
    cot_half = lax.dynamic_slice_in_dim(out_cotangent, mine, half_rows)
    cot = lax.all_gather(cot_half, TEAM, axis=0, tiled=True)

    gate = dot(normed2, gate_full)
    up_val = dot(normed2, up_full)
    sigma = jax.nn.sigmoid(gate)
    silu_val = gate * sigma
    act = (silu_val * up_val).astype(BF16)
    ffn_part = contract_last(act, down_full).astype(BF16)
    d_act = dot(cot, down_full)
    d_gate = (d_act * up_val * sigma * (1.0 + gate * (1.0 - sigma))).astype(BF16)
    d_up = (d_act * silu_val).astype(BF16)
    dn2_part = (contract_last(d_gate, gate_full) + contract_last(d_up, up_full)).astype(BF16)
    ffn_half = lax.psum_scatter(ffn_part, TEAM, scatter_dimension=0, tiled=True)
    block_half = (resid_half + ffn_half.astype(F32)).astype(BF16)
    block_out = lax.all_gather(block_half, "tensor", axis=0, tiled=True)
    dn2_half = lax.psum_scatter(dn2_part, TEAM, scatter_dimension=0, tiled=True).astype(F32)
    grad_g2, d_back2 = norm_backward(dn2_half, unit2, factor2, gain_two)
    d_resid_half = cot_half.astype(F32) + d_back2

    def give_back(grad):
        part = lax.psum_scatter(grad.astype(BF16), "shard", scatter_dimension=0, tiled=True)
        part = part.reshape(blocks, depth, unit_cols)
        part = lax.all_to_all(part, "context", split_axis=0, concat_axis=2, tiled=True)
        return part.reshape(depth, padded)[:, :hidden_units].astype(F32)

    sum_gate = give_back(contract_first(normed2, d_gate))
    sum_up = give_back(contract_first(normed2, d_up))
    sum_down = give_back(contract_first(cot, act)).T

    d_resid_b = lax.all_gather(d_resid_half.astype(BF16), "tensor", axis=0, tiled=True)
    grad_out = contract_first(d_resid_b, attn)
    d_attn = dot(d_resid_b, out_full).astype(BF16)
    d_outs = jnp.transpose(d_attn.reshape(rows, heads, HD), (1, 0, 2)).reshape(
        kv, repeat * rows, HD
    )
    d_prob = batched(d_outs, values, 2, 2)
    delta = jnp.sum(d_outs.astype(F32) * outs.astype(F32), axis=2, keepdims=True)
    d_score = (p_soft * (d_prob - delta)).astype(BF16)
    d_query = batched(d_score, keys, 2, 1) * scale
    d_keys = batched(d_score, query, 1, 1) * scale
    d_values = batched(probs, d_outs, 1, 1)
    d_kv = jnp.concatenate([d_keys, d_values], axis=0).astype(BF16)
    d_kv = lax.psum_scatter(d_kv, "context", scatter_dimension=1, tiled=True).astype(F32)
    d_query = unrotate(d_query.reshape(heads, rows, HD), cos_local, sin_local)
    d_keys = unrotate(d_kv[:kv], cos_local, sin_local)
    d_proj = jnp.transpose(jnp.concatenate([d_query, d_keys, d_kv[kv:]], axis=0), (1, 0, 2))
    grad_bias = jnp.sum(d_proj, axis=0)
    d_projb = d_proj.reshape(rows, -1).astype(BF16)
    grad_qkv = contract_first(normed1, d_projb)
    dn1_part = contract_last(d_projb, qkv_full).astype(BF16)
    dn1_half = lax.psum_scatter(dn1_part, "tensor", scatter_dimension=0, tiled=True).astype(F32)
    unit1_half = lax.dynamic_slice_in_dim(unit1, mine, half_rows)
    factor1_half = lax.dynamic_slice_in_dim(factor1, mine, half_rows)
    grad_g1, d_back1 = norm_backward(dn1_half, unit1_half, factor1_half, gain_one)
    input_grad = lax.all_gather(d_resid_half + d_back1, "tensor", axis=0, tiled=True)

    gains = lax.psum(jnp.stack([grad_g1, grad_g2]), "tensor")
    sum_gains = lax.psum_scatter(gains, OWNERS, scatter_dimension=1, tiled=True)
    sum_qkv = lax.psum_scatter(grad_qkv.astype(BF16), OWNERS, scatter_dimension=0, tiled=True)
    sum_bias = lax.psum_scatter(grad_bias, OWNERS, scatter_dimension=1, tiled=True)
    sum_out = lax.psum_scatter(grad_out.astype(BF16), OWNERS, scatter_dimension=0, tiled=True)
    return (
        block_out,
        input_grad,
        sum_gains[0],
        sum_qkv.astype(F32),
        sum_bias,
        sum_out.astype(F32).T,
        sum_gains[1],
        sum_gate,
        sum_up,
        sum_down,
    )


def solution(mesh):
    ns, nz, parts = (mesh.shape[a] for a in ("shard", "context", "tensor"))
    rows = P(OWNERS, None)

    def local(*args):
        depth = args[7].shape[0]
        if depth % SUBLANES == 0 and ns % 2 == 0 and ns > 2 and nz > 1 and parts == 2:
            return fast_step(ns, nz, *args)
        return general_step(*args)

    placed = (
        rows,
        P("shard", None),
        P(OWNERS),
        P(OWNERS, "tensor"),
        P("tensor", OWNERS),
        P("tensor", OWNERS),
        P(OWNERS),
        P(OWNERS, "tensor"),
        P(OWNERS, "tensor"),
        P("tensor", OWNERS),
        rows,
    )
    return jax.shard_map(
        local,
        mesh=mesh,
        in_specs=placed,
        out_specs=(
            rows,
            rows,
            P(OWNERS),
            P(OWNERS, "tensor"),
            P("tensor", OWNERS),
            P("tensor", OWNERS),
            P(OWNERS),
            P(OWNERS, "tensor"),
            P(OWNERS, "tensor"),
            P("tensor", OWNERS),
        ),
        check_vma=False,
    )
```

time: 1660 us -> 756 us (0.46)
  waiting for transfers between devices: 1280 us -> 399 us
  Pallas kernels: 0 us -> 157 us
  matrix products: 147 us -> 53.4 us
  blocking collectives: 151 us -> 66.8 us
    reduce_scatter x6 -> x9, waiting for transfers between devices: 913 us -> 340 us  [the longest x1 68.1 us: fast_step(): lax.psum_scatter(dn2_part, TEAM, scatter_dimension=0, tiled=True)]
    all_gather x5 -> x0, waiting for transfers between devices: 305 us -> none  [the longest x1 105 us: local(): lax.all_gather(gate_weight, ('shard', 'context'), axis=0, tiled=True)]
    pallas_call x0 -> x1, Pallas kernels: none -> 157 us  [front(): pl.pallas_call(functools.partial(front_kernel, ns, nz, heads, kv), out_sh...]
    unnamed x2 -> x1, blocking collectives: 95.3 us -> 40.6 us
    psum x3 -> x0, waiting for transfers between devices: 50.8 us -> none  [the longest x1 26 us: local(): lax.psum((contract_last(d_gate, gate_full) + contract_last(d_up, up_full)...]
    dot_general x17 -> x5, matrix products: 59.5 us -> 22.4 us  [contract_first(): lax.dot_general(left, right, (((0,), (0,)), ((), ())), preferred_element_...]
    unnamed x16 -> x11, waiting for transfers between devices: 7.3 us -> 44.1 us
    all_gather x3, blocking collectives: 55.4 us -> 21.2 us  [the longest x1 8.43 us: fast_step(): lax.all_gather(d_resid_half + d_back1, 'tensor', axis=0, tiled=True)]
  transfers between devices with their start and end apart: 15 -> 13, of which waited for: 12 -> 9; matrix products, arithmetic and copies ran while one was open for 7% -> 7% of each run, Pallas kernels for 0% -> 0%
where the time goes in v1:
time: 756 us; the launch traced here: 750 us
  waiting for transfers between devices  399 us (53%)
  Pallas kernels  157 us (21%)
  blocking collectives  66.8 us (9%)
  matrix products  53.4 us (7%)
  other arithmetic  21.4 us (3%)
  local copies, waits for them, and re-layouts  19.3 us (3%)
  starting transfers between devices  17.8 us (2%)
  between operations  15.5 us (2%)
    pallas_call x1, Pallas kernels, front(): pl.pallas_call(functools.partial(front_kernel, ns, nz, heads, kv), out_sh...  157 us
    reduce_scatter x1, waiting for transfers between devices, fast_step(): lax.psum_scatter(dn2_part, TEAM, scatter_dimension=0, tiled=True)  68.1 us
    reduce_scatter x1, waiting for transfers between devices, fast_step(): lax.psum_scatter(grad_qkv.astype(BF16), OWNERS, scatter_dimension=0, tile...  67.3 us
    reduce_scatter x1, waiting for transfers between devices, fast_step(): ffn_half = lax.psum_scatter(ffn_part, TEAM, scatter_dimension=0, tiled=True)  66 us
    reduce_scatter x3, waiting for transfers between devices, give_back(): lax.psum_scatter(grad.astype(BF16), 'shard', scatter_dimension=0, tiled=T...  62.9 us
    reduce_scatter x1, waiting for transfers between devices, fast_step(): lax.psum_scatter(grad_out.astype(BF16), OWNERS, scatter_dimension=0, tile...  59.6 us
    unnamed x11, waiting for transfers between devices  44.1 us
    unnamed x1, blocking collectives  40.6 us
  transfers between devices with their start and end apart: 13, of which 9 were waited for; matrix products, arithmetic and copies ran while one was open for 7% of the time, Pallas kernels for 0%

profile of v1, /device:TPU:10, one launch (start us, length us, event | category | flops | bytes accessed | tf_op | source)
XLA Modules:
  0.0 750.1 jit_solution(8471458724769099831)
XLA Ops:
  7.3 1.3 pad.20
  8.6 1.0 copy.83
  10.0 0.9 fusion.38
  13.9 1.3 bitcast_bitcast_fusion
  15.9 156.5 %shard_map.186 = (bf16[1536,1792]{1,0:T(8,128)(2,1)}, bf16[1536,1152]{1,0:T(8,128)(2,1)}, bf16[1536,1152]{1,0:T(8,128)(2,1)}, bf16[1536,1152]{1,0:T(8,128)(2,1)}...) custom-call(bf16[96,1792]{1,0:T(8,128)(2,1)} %pad_maximum_fusion.ref, ...), custom_call_target="tpu_custom_call" | custom-call | tf_op jit(solution)/shard_map/pallas_call | solution.py:408
  172.5 4.8 fusion.52
  177.3 2.2 fusion.53
  179.8 3.8 multiply_convert_fusion
  183.6 2.4 fusion.54
  186.1 3.4 fusion.2
  192.7 1.1 fusion.50
  193.7 68.1 %reduce-scatter.16.cloned.1.call-done = bf16[64,1536]{1,0:T(8,128)(2,1)} async-done(((bf16[512,1536]{1,0:T(8,128)(2,1)}), bf16[64,1536]{1,0:T(8,128)(2,1)}) %reduce-scatter.16.cloned.1.call-update) | async-done | bytes 196624 | tf_op jit(solution)/shard_map/reduce_scatter | solution.py:525
  261.9 1.7 fusion.27
  263.6 1.1 fusion.48
  264.6 6.3 all_gather.10
  271.7 2.3 fusion.9
  274.9 1.3 multiply_convert_fusion.3
  278.1 15.8 %reduce-scatter.18.cloned.1.call-done = bf16[2,128,128]{2,1,0:T(8,128)(2,1)} async-done(((bf16[2,512,128]{2,1,0:T(8,128)(2,1)}), bf16[2,128,128]{2,1,0:T(8,128)(2,1)}) %reduce-scatter.18.cloned.1.call-update) | async-done | bytes 65552 | tf_op jit(solution)/shard_map/reduce_scatter | solution.py:552
  296.8 3.8 fusion.3
  300.7 5.8 convolution_convert_fusion.2
  306.5 5.8 convolution_convert_fusion.1
  312.6 5.8 convolution_convert_fusion.5
  319.1 1.6 fusion.28
  320.8 1.2 copy.66
  322.1 2.2 convolution_convert_fusion.4
  324.3 2.7 convolution_convert_fusion.3
  327.2 6.0 convolution_convert_fusion
  333.2 23.9 %reduce-scatter.26.cloned.1.call-done = bf16[384,1152]{1,0:T(8,128)(2,1)} async-done(((bf16[1536,1152]{1,0:T(8,128)(2,1)}), bf16[384,1152]{1,0:T(8,128)(2,1)}) %reduce-scatter.26.cloned.1.call-update) | async-done | bytes 884752 | tf_op jit(solution)/shard_map/reduce_scatter | solution.py:530
  357.1 5.1 all-to-all-start
  364.3 40.6 %all-reduce.5 = f32[8,128]{1,0:T(8,128)S(1)} all-reduce(f32[8,128]{1,0:T(8,128)S(1)} %fusion.31), channel_id=8, replica_groups=mesh['shard'=4,'context'=4,'tensor'=2] {'shard','context'}, use_global_device_ids=true, to_apply=%region_16.17.clone | all-reduce | flops 1024 | bytes 8192
  405.6 6.9 all-to-all-start.1
  412.5 1.2 broadcast_multiply_fusion
  413.6 66.0 %reduce-scatter.14.cloned.1.call-done = bf16[64,1536]{1,0:T(8,128)(2,1)} async-done(((bf16[512,1536]{1,0:T(8,128)(2,1)}), bf16[64,1536]{1,0:T(8,128)(2,1)}) %reduce-scatter.14.cloned.1.call-update) | async-done | bytes 196624 | tf_op jit(solution)/shard_map/reduce_scatter | solution.py:522
  479.6 1.3 fusion.23
  481.0 6.4 all_gather.9
  487.4 8.4 %all_gather.11 = f32[128,1536]{1,0:T(8,128)S(1)} all-gather(f32[64,1536]{1,0:T(8,128)S(1)} %get-tuple-element.43), channel_id=1, replica_groups=mesh['shard'=4,'context'=4,'tensor'=2] {'tensor'}, dimensions={0}, use_global_device_ids=true | all-gather | bytes 1179648 | tf_op jit(solution)/shard_map/all_gather | solution.py:564
  495.8 43.9 %reduce-scatter.32.cloned.1.call-done = f32[96,2]{1,0:T(8,128)} async-done(((f32[1536,2]{1,0:T(8,128)}), f32[96,2]{1,0:T(8,128)}) %reduce-scatter.32.cloned.1.call-update) | async-done | bytes 784
  540.6 4.9 psum.8
  546.1 59.6 %reduce-scatter.24.cloned.1.call-done = bf16[96,768]{1,0:T(8,128)(2,1)} async-done(((bf16[1536,768]{1,0:T(8,128)(2,1)}), bf16[96,768]{1,0:T(8,128)(2,1)}) %reduce-scatter.24.cloned.1.call-update) | async-done | bytes 147472 | tf_op jit(solution)/shard_map/reduce_scatter | solution.py:570
  605.7 1.6 convert_bitcast_fusion.1
  607.4 67.3 %reduce-scatter.22.cloned.1.call-done = bf16[96,1024]{1,0:T(8,128)(2,1)} async-done(((bf16[1536,1024]{1,0:T(8,128)(2,1)}), bf16[96,1024]{1,0:T(8,128)(2,1)}) %reduce-scatter.22.cloned.1.call-update) | async-done | bytes 196624 | tf_op jit(solution)/shard_map/reduce_scatter | solution.py:568
  674.7 1.7 convert_element_type.156
  676.9 39.0 %reduce-scatter.30.cloned.1.call-done = bf16[384,1152]{1,0:T(8,128)(2,1)} async-done(((bf16[1536,1152]{1,0:T(8,128)(2,1)}), bf16[384,1152]{1,0:T(8,128)(2,1)}) %reduce-scatter.30.cloned.1.call-update) | async-done | bytes 884752 | tf_op jit(solution)/shard_map/reduce_scatter | solution.py:530
  715.9 5.1 all-to-all-start.2
  721.0 1.3 slice_convert_fusion.1
  722.9 1.3 slice_convert_fusion
  724.2 15.6 %all-to-all-done.2 = bf16[4,96,1152]{2,1,0:T(8,128)(2,1)S(1)} async-done(((bf16[4,96,1152]{2,1,0:T(8,128)(2,1)}), bf16[4,96,1152]{2,1,0:T(8,128)(2,1)S(1)}, u32[]{:S(2)}, u32[]{:S(2)}) %all-to-all-start.2) | async-done | bytes 884768 | tf_op jit(solution)/shard_map/all_to_all | solution.py:532
  740.4 1.3 convert_bitcast_fusion
  (165 shorter events, 21.7 us)
Async XLA Ops:
  7.2 2.4 copy-start.9
  7.2 254.7 %reduce-scatter.16.cloned.1.call-start = ((), (), s32[]{:S(2)}) async-start(), calls=%async_computation.14 | async-start | bytes 1769472 | tf_op jit(solution)/shard_map/reduce_scatter | solution.py:525
  7.3 2.4 copy-start.10
  9.6 2.9 copy-start.24
  9.6 2.9 copy-start.25
  9.6 3.6 copy-start.31
  9.6 3.6 copy-start.32
  9.6 3.6 copy-start.29
  172.5 4.8 copy-start.34
  172.5 4.8 copy-start.37
  177.3 2.2 copy-start.33
  177.3 2.5 copy-start.36
  179.8 3.8 copy-start.35
  183.6 2.4 copy-start.39
  183.6 2.4 copy-start.40
  186.1 3.5 copy-start.13
  186.1 4.2 copy-start.14
  186.1 4.9 copy-start.11
  189.5 3.0 copy-start.2
  189.5 74.1 %copy-start.5 = (bf16[128,1536]{1,0:T(8,128)(2,1)S(1)}, bf16[128,1536]{1,0:T(8,128)(2,1)}, u32[]{:S(2)}) copy-start(bf16[128,1536]{1,0:T(8,128)(2,1)} %refs_6_.1) | copy-start | bytes 1179652
  189.5 104.4 %reduce-scatter.18.cloned.1.call-start = ((), (), s32[]{:S(2)}) async-start(), calls=%async_computation.15 | async-start | bytes 327680 | tf_op jit(solution)/shard_map/reduce_scatter | solution.py:552
  192.7 78.3 %copy-start.28 = (f32[64]{0:T(128)}, f32[64]{0:T(128)S(1)}, u32[]{:S(2)}) copy-start(f32[64]{0:T(128)S(1)} %add_rsqrt_fusion.1) | copy-start | bytes 772
  263.6 7.4 copy-start.30
  271.7 2.7 copy-start.1
  276.2 1.8 copy-start.20
  276.2 1.8 copy-start.21
  277.4 41.7 %reduce-scatter.20.cloned.1.call-start = ((), (), s32[]{:S(2)}) async-start(), calls=%async_computation.16 | async-start | bytes 589824 | tf_op jit(solution)/shard_map/reduce_scatter | solution.py:560
  277.4 19.1 %copy-start.19 = (f32[1,128,64]{2,1,0:T(8,128)S(1)}, f32[1,128,64]{2,1,0:T(8,128)}, u32[]{:S(2)}) copy-start(f32[1,128,64]{2,1,0:T(8,128)} %get-tuple-element.55) | copy-start | bytes 98308
  294.7 5.9 copy-start.15
  296.7 3.9 copy-start.17
  300.6 56.5 %reduce-scatter.26.cloned.1.call-start = ((), (), s32[]{:S(2)}) async-start(), calls=%async_computation.19 | async-start | bytes 4423680 | tf_op jit(solution)/shard_map/reduce_scatter | solution.py:530
  306.5 99.1 %reduce-scatter.28.cloned.1.call-start = ((), (), s32[]{:S(2)}) async-start(), calls=%async_computation.20 | async-start | bytes 4423680 | tf_op jit(solution)/shard_map/reduce_scatter | solution.py:530
  312.3 167.3 %reduce-scatter.14.cloned.1.call-start = ((), (), s32[]{:S(2)}) async-start(), calls=%async_computation.13 | async-start | bytes 1769472 | tf_op jit(solution)/shard_map/reduce_scatter | solution.py:522
  312.6 5.9 copy-start
  318.4 3.6 copy-start.8
  318.4 3.6 copy-start.12
  318.4 221.3 %reduce-scatter.32.cloned.1.call-start = ((), (), s32[]{:S(2)}) async-start(), calls=%async_computation.22 | async-start | bytes 835584
  322.0 283.7 %reduce-scatter.24.cloned.1.call-start = ((), (), s32[]{:S(2)}) async-start(), calls=%async_computation.18 | async-start | bytes 2506752 | tf_op jit(solution)/shard_map/reduce_scatter | solution.py:570
  324.3 350.4 %reduce-scatter.22.cloned.1.call-start = ((), (), s32[]{:S(2)}) async-start(), calls=%async_computation.17 | async-start | bytes 3342336 | tf_op jit(solution)/shard_map/reduce_scatter | solution.py:568
  327.1 388.8 %reduce-scatter.30.cloned.1.call-start = ((), (), s32[]{:S(2)}) async-start(), calls=%async_computation.21 | async-start | bytes 4423680 | tf_op jit(solution)/shard_map/reduce_scatter | solution.py:530
  333.1 29.7 %copy-start.38 = (u32[32]{0:T(128)S(1)}, u32[32]{0:T(128)}, u32[]{:S(2)}) copy-start(u32[32]{0:T(128)} %constant.57) | copy-start | bytes 388
  333.1 30.9 %copy-start.16 = (f32[1,128,128]{1,2,0:T(8,128)S(1)}, f32[1,128,128]{1,2,0:T(8,128)}, u32[]{:S(2)}) copy-start(f32[1,128,128]{1,2,0:T(8,128)} %copy-done.15) | copy-start | bytes 196612
  333.1 30.9 %copy-start.18 = (f32[1,128,128]{1,2,0:T(8,128)S(1)}, f32[1,128,128]{1,2,0:T(8,128)}, u32[]{:S(2)}) copy-start(f32[1,128,128]{1,2,0:T(8,128)} %copy-done.17) | copy-start | bytes 196612
  333.1 146.5 %copy-start.3 = (bf16[64,1536]{1,0:T(8,128)(2,1)S(1)}, bf16[64,1536]{1,0:T(8,128)(2,1)}, u32[]{:S(2)}) copy-start(bf16[64,1536]{1,0:T(8,128)(2,1)} %reduce-scatter.16.cloned.1.call-done) | copy-start | bytes 589828
  333.2 146.5 %copy-start.6 = (bf16[128,1536]{1,0:T(8,128)(2,1)S(1)}, bf16[128,1536]{1,0:T(8,128)(2,1)}, u32[]{:S(2)}) copy-start(bf16[128,1536]{1,0:T(8,128)(2,1)} %refs_6_.1) | copy-start | bytes 1179652
  357.1 48.5 %all-to-all-start = ((bf16[4,96,1152]{2,1,0:T(8,128)(2,1)}), bf16[4,96,1152]{2,1,0:T(8,128)(2,1)S(1)}, u32[]{:S(2)}, u32[]{:S(2)}) async-start(bf16[4,96,1152]{2,1,0:T(8,128)(2,1)} %bitcast.147), calls=%async_computation.7 | async-start | bytes 1769472 | tf_op jit(solution)/shard_map/all_to_all | solution.py:532
  405.6 310.3 %all-to-all-start.1 = ((bf16[4,96,1152]{2,1,0:T(8,128)(2,1)}), bf16[4,96,1152]{2,1,0:T(8,128)(2,1)S(1)}, u32[]{:S(2)}, u32[]{:S(2)}) async-start(bf16[4,96,1152]{2,1,0:T(8,128)(2,1)} %bitcast.146), calls=%async_computation.9 | async-start | bytes 1769472 | tf_op jit(solution)/shard_map/all_to_all | solution.py:532
  715.9 23.9 %all-to-all-start.2 = ((bf16[4,96,1152]{2,1,0:T(8,128)(2,1)}), bf16[4,96,1152]{2,1,0:T(8,128)(2,1)S(1)}, u32[]{:S(2)}, u32[]{:S(2)}) async-start(bf16[4,96,1152]{2,1,0:T(8,128)(2,1)} %bitcast.148), calls=%async_computation.11 | async-start | bytes 1769472 | tf_op jit(solution)/shard_map/all_to_all | solution.py:532
  (6 other events, 7.5 us)
Sparse Core Ops, SparseCore 0:
  189.6 72.2 reduce-scatter.15
  277.5 16.3 reduce-scatter.17
  300.8 14.3 reduce-scatter.19
  317.6 39.4 reduce-scatter.25
  359.5 40.3 reduce-scatter.27
  403.8 75.8 reduce-scatter.13
  483.8 55.9 reduce-scatter.31
  543.5 62.1 reduce-scatter.23
  609.5 65.0 reduce-scatter.21
  677.1 38.7 reduce-scatter.29

commit v2 on v1

--- a/solution.py
+++ b/solution.py
@@ -102,11 +102,17 @@
     def mate_from(self, o):
         return lax.rem(self.outer - o + self.no, self.no) * 2 + 1 - self.core
 
-    def greet(self):
+    def mate_to(self, o):
+        return lax.rem(self.outer + o, self.no) * 2 + 1 - self.core
+
+    def greet(self, everyone=False):
         barrier = pltpu.get_barrier_semaphore()
         peers = [{"context": self.z_to(d)} for d in range(1, self.nz)]
-        peers += [{"shard": self.s_to(o)} for o in range(1, self.no)]
-        peers += [{"shard": self.mate}, {"tensor": self.twin}]
+        if everyone:
+            peers += [{"shard": lax.rem(self.s + k, self.ns)} for k in range(1, self.ns)]
+        else:
+            peers += [{"shard": self.s_to(o)} for o in range(1, self.no)] + [{"shard": self.mate}]
+        peers += [{"tensor": self.twin}]
         for peer in peers:
             pl.semaphore_signal(barrier, inc=1, device_id=peer, device_id_type=MESH)
         pl.semaphore_wait(barrier, len(peers))
@@ -435,6 +441,462 @@
     )(wa_in, small_in, *ffn_in, hidden, cot, cosine, sine, mask)
 
 
+def ffn_kernel(gate_in, up_in, down_in, n2, cot, act, d_gate, d_up, ffn_part, dn2_part, *scratch):
+    gate_w, up_w, down_w, gate, up_val, d_act, sem = scratch
+    loads = [
+        pltpu.make_async_copy(src, dst, sem.at[i])
+        for i, (src, dst) in enumerate(((gate_in, gate_w), (up_in, up_w), (down_in, down_w)))
+    ]
+    for load in loads:
+        load.start()
+    for load, left, weight, out in zip(loads, (n2, n2, cot), (gate_w, up_w, down_w), (gate, up_val, d_act)):
+        load.wait()
+        out[...] = jnp.dot(left[...], weight[...], preferred_element_type=F32)
+
+    tall = 32
+
+    @pl.loop(0, gate.shape[0] // tall)
+    def _(i):
+        line = pl.ds(pl.multiple_of(i * tall, tall), tall)
+        g, u, d = gate[line, :], up_val[line, :], d_act[line, :]
+        sigma = jax.nn.sigmoid(g)
+        silu_val = g * sigma
+        act[line, :] = (silu_val * u).astype(BF16)
+        d_gate[line, :] = (d * u * sigma * (1.0 + g * (1.0 - sigma))).astype(BF16)
+        d_up[line, :] = (d * silu_val).astype(BF16)
+
+    def back(left, weight):
+        return lax.dot_general(
+            left[...], weight[...], (((1,), (1,)), ((), ())), preferred_element_type=F32
+        )
+
+    dn2_part[...] = (back(d_gate, gate_w) + back(d_up, up_w)).astype(BF16)
+    ffn_part[...] = back(act, down_w).astype(BF16)
+
+
+def ffn(gate_w, up_w, down_w, n2, cot):
+    rows, width = n2.shape
+    unit = gate_w.shape[1]
+    shape = jax.ShapeDtypeStruct
+    vmem = pl.BlockSpec(memory_space=pltpu.VMEM)
+    anyspace = pl.BlockSpec(memory_space=pl.ANY)
+    return pl.pallas_call(
+        ffn_kernel,
+        out_shape=[shape((rows, unit), BF16)] * 3 + [shape((rows, width), BF16)] * 2,
+        in_specs=[anyspace] * 3 + [vmem] * 2,
+        out_specs=[vmem] * 5,
+        scratch_shapes=[pltpu.VMEM((width, unit), BF16)] * 3
+        + [pltpu.VMEM((rows, unit), F32)] * 3
+        + [pltpu.SemaphoreType.DMA((3,))],
+        compiler_params=pltpu.CompilerParams(vmem_limit_bytes=VMEM_BYTES),
+    )(gate_w, up_w, down_w, n2, cot)
+
+
+def turn_first(left, right):
+    return lax.dot_general(left, right, (((0,), (0,)), ((), ())), preferred_element_type=F32)
+
+
+def turn_last(left, right):
+    return lax.dot_general(left, right, (((1,), (1,)), ((), ())), preferred_element_type=F32)
+
+
+class Return:
+    def __init__(self, at, sends, make, bufs, out, sems):
+        self.at, self.sends, self.make, self.out = at, sends, make, out
+        self.stage, self.acc, self.landc, self.landx = bufs
+        self.cs, self.cr, self.xs, self.xr, self.zs, self.zr, self.own = sems
+        self.depth = self.acc.shape[1] // at.nz
+        self.copy = None
+
+    @staticmethod
+    def sems(ns, nz):
+        dma, no = pltpu.SemaphoreType.DMA, ns // 2
+        return [dma((no,)), dma((no,)), dma((no,)), dma((no,)), dma((nz,)), dma((nz,)), dma]
+
+    @staticmethod
+    def bufs(ns, nz, depth, cols):
+        no = ns // 2
+        return [pltpu.VMEM((n, nz * depth, cols), BF16) for n in (no, no, no, no)]
+
+    def give(self, o):
+        at = self.at
+        self.stage[o] = self.make(at.mate_to(o)).astype(BF16)
+        self.sends.go(
+            self.stage.at[o], self.landc.at[o], self.cs.at[o], self.cr.at[o], shard=at.mate
+        )
+        self.acc[o] = self.make(at.s_to(o)).astype(BF16)
+
+    def give_all(self):
+        for o in (*range(1, self.at.no), 0):
+            self.give(o)
+
+    def add(self, o, others):
+        @pl.loop(0, self.at.nz)
+        def _(i):
+            line = pl.ds(pl.multiple_of(i * self.depth, SUBLANES), self.depth)
+            total = self.acc[o, line, :].astype(F32)
+            for other, k in others:
+                total = total + other[k, line, :].astype(F32)
+            self.acc[o, line, :] = total.astype(BF16)
+
+    def over_s(self):
+        at = self.at
+        for o in range(1, at.no):
+            landed(self.landc.at[o], self.cs.at[o], self.cr.at[o], shard=at.mate)
+            self.add(o, [(self.landc, o)])
+            self.sends.go(
+                self.acc.at[o], self.landx.at[o], self.xs.at[o], self.xr.at[o], shard=at.s_to(o)
+            )
+
+    def piece(self, z2):
+        return self.acc.at[0, pl.ds(pl.multiple_of(z2 * self.depth, SUBLANES), self.depth)]
+
+    def over_z(self):
+        at = self.at
+        landed(self.landc.at[0], self.cs.at[0], self.cr.at[0], shard=at.mate)
+        for o in range(1, at.no):
+            landed(self.landx.at[o], self.xs.at[o], self.xr.at[o], shard=at.s_from(o))
+        self.add(0, [(self.landc, 0)] + [(self.landx, o) for o in range(1, at.no)])
+        for d in range(1, at.nz):
+            z2 = at.z_to(d)
+            self.sends.go(
+                self.piece(z2), self.out.at[at.z], self.zs.at[d], self.zr.at[d], context=z2
+            )
+        self.copy = pltpu.make_async_copy(self.piece(at.z), self.out.at[at.z], self.own)
+        self.copy.start()
+
+    def finish(self):
+        at = self.at
+        self.copy.wait()
+        for d in range(1, at.nz):
+            z1 = at.z_from(d)
+            landed(self.out.at[z1], self.zs.at[d], self.zr.at[d], context=z1)
+
+
+class Reduce:
+    def __init__(self, at, sends, parts, bufs, sems):
+        self.at, self.sends, self.parts = at, sends, parts
+        self.landy, self.stage, self.landz = bufs
+        self.ys, self.yr, self.zs, self.zr = sems
+        self.own = None
+
+    @staticmethod
+    def sems(nz):
+        dma = pltpu.SemaphoreType.DMA
+        return [dma((nz,)), dma((nz,)), dma((nz,)), dma((nz,))]
+
+    @staticmethod
+    def bufs(nz, half, width):
+        return [pltpu.VMEM((nz, half, width), BF16)] * 3
+
+    def over_y(self):
+        at = self.at
+        for d in (*range(1, at.nz), 0):
+            self.sends.go(
+                self.parts.at[at.z_to(d), at.twin], self.landy.at[d], self.ys.at[d],
+                self.yr.at[d], tensor=at.twin,
+            )
+
+    def pass_y(self):
+        at = self.at
+        for d in (*range(1, at.nz), 0):
+            landed(self.landy.at[d], self.ys.at[d], self.yr.at[d], tensor=at.twin)
+            total = self.parts[at.z_to(d), at.y].astype(F32) + self.landy[d].astype(F32)
+            self.stage[d] = total.astype(BF16)
+            if d:
+                self.sends.go(
+                    self.stage.at[d], self.landz.at[d], self.zs.at[d], self.zr.at[d],
+                    context=at.z_to(d),
+                )
+
+    def total(self):
+        at = self.at
+        total = self.stage[0].astype(F32)
+        for d in range(1, at.nz):
+            landed(self.landz.at[d], self.zs.at[d], self.zr.at[d], context=at.z_from(d))
+            total = total + self.landz[d].astype(F32)
+        return total
+
+
+def piece_of_lines(lines, b, depth):
+    first, off = divmod(b * depth, LANES)
+    tile = lines[:, first * LANES:(first + 1) * LANES]
+    if not off:
+        return tile
+    tile = pltpu.roll(tile, LANES - off, 1)
+    if off + depth <= LANES:
+        return tile
+    after = pltpu.roll(lines[:, (first + 1) * LANES:(first + 2) * LANES], LANES - off, 1)
+    lane = lax.broadcasted_iota(jnp.int32, (8, LANES), 1)
+    return jnp.where(lane < LANES - off, tile, after)
+
+
+N_BACK_IN = 18
+
+
+def back_kernel(ns, nz, heads, kv, *refs):
+    ins, refs = refs[:N_BACK_IN], refs[N_BACK_IN:]
+    (wa_in, n2_in, cot_in, act_in, d_gate_in, d_up_in, probs_in, dn2_part, ffn_part, hidden, resid,
+     cot_own, lines, query, kv_all, attn, cosine, sine) = ins
+    (block_out, input_grad, attn_grad, small_out, *ffn_out), refs = refs[:7], refs[7:]
+    (wa, n2, cot, act, d_gate, d_up, probs), refs = refs[:7], refs[7:]
+    fetch_sem, refs = refs[0], refs[1:]
+    at, sends = Place(ns, nz), Sends()
+    depth = lines.shape[1] // (ns * nz)
+    rows, width = hidden.shape
+    half = rows // 2
+    group_rows = nz * rows
+    q_cols = heads * HD
+    qkv_cols = q_cols + 2 * kv * HD
+    wide = nz * depth
+    scale = HD ** (-0.5)
+    n_ret, n_red = len(Return.sems(ns, nz)), len(Reduce.sems(nz))
+
+    loads = {}
+    for i, (name, src, dst) in enumerate((
+        ("n2", n2_in, n2), ("d_gate", d_gate_in, d_gate), ("d_up", d_up_in, d_up),
+        ("cot", cot_in, cot), ("act", act_in, act), ("wa", wa_in, wa), ("probs", probs_in, probs),
+    )):
+        loads[name] = pltpu.make_async_copy(src, dst, fetch_sem.at[i])
+        loads[name].start()
+
+    def columns(ref, s1):
+        return ref[:, pl.ds(pl.multiple_of(s1 * wide, LANES), wide)]
+
+    rets = []
+    makers = (
+        lambda s1: turn_first(columns(n2, s1), d_gate[...]),
+        lambda s1: turn_first(columns(n2, s1), d_up[...]),
+        lambda s1: turn_first(columns(cot, s1), act[...]),
+    )
+    for i in range(3):
+        bufs, sems, refs = refs[:4], refs[4:4 + n_ret], refs[4 + n_ret:]
+        rets.append(Return(at, sends, makers[i], bufs, ffn_out[i], sems))
+    bufs, sems, attn_land, refs = refs[:4], refs[4:4 + n_ret], refs[4 + n_ret], refs[5 + n_ret:]
+    normed1_b, d_resid_b, d_projb, refs = refs[0], refs[1], refs[2], refs[3:]
+
+    def attn_maker(s1):
+        grad_qkv = turn_first(columns(normed1_b, s1), d_projb[...])
+        both = d_resid_b[:, :, pl.ds(pl.multiple_of(s1 * wide, LANES), wide)].reshape(rows, wide)
+        grad_out = turn_first(both, attn[...])
+        return jnp.concatenate([grad_qkv, grad_out], axis=1)
+
+    r_attn = Return(at, sends, attn_maker, bufs, attn_land, sems)
+    reduces = []
+    for parts in (dn2_part, ffn_part):
+        bufs, sems, refs = refs[:3], refs[3:3 + n_red], refs[3 + n_red:]
+        reduces.append(Reduce(at, sends, parts, bufs, sems))
+    r_dn2, r_ffn = reduces
+    (d_resid_f, d_attn, d_score, dkv, dkv_land, dn1_part, dn1_land, small, small_land, small_z,
+     small_zland, small_y, small_yland, dkvs, dkvr, shs, shr, szs, szr, ysems, yrecv) = refs
+
+    at.greet(everyone=True)
+    r_dn2.over_y()
+    loads["n2"].wait()
+    loads["d_gate"].wait()
+    rets[0].give_all()
+    r_dn2.pass_y()
+    r_ffn.over_y()
+    loads["d_up"].wait()
+    rets[1].give_all()
+    rets[0].over_s()
+
+    res = resid[...]
+    factor2 = lax.rsqrt(jnp.mean(res * res, axis=1, keepdims=True) + EPSILON)
+    unit2 = res * factor2
+    dn2 = r_dn2.total()
+    grad_g2 = jnp.sum(dn2 * unit2, axis=0, keepdims=True)
+    scaled = dn2 * lines[1:2, :]
+    back2 = factor2 * (scaled - unit2 * jnp.mean(scaled * unit2, axis=1, keepdims=True))
+    base = pl.multiple_of(at.y * half, SUBLANES)
+    d_res = cot_own[pl.ds(base, half), :].astype(F32) + back2
+    d_resid_f[at.y] = d_res
+    d_resid_b[at.y] = d_res.astype(BF16)
+    mine_b, mine_f = d_resid_b.at[at.y], d_resid_f.at[at.y]
+    sends.go(mine_b, mine_b, ysems.at[0], yrecv.at[0], tensor=at.twin)
+    sends.go(mine_f, mine_f, ysems.at[1], yrecv.at[1], tensor=at.twin)
+
+    loads["cot"].wait()
+    loads["act"].wait()
+    rets[2].give_all()
+    rets[1].over_s()
+    r_ffn.pass_y()
+    hidden_f = hidden[...].astype(F32)
+    factor1 = lax.rsqrt(jnp.mean(hidden_f * hidden_f, axis=1, keepdims=True) + EPSILON)
+    normed1_b[...] = (hidden_f * factor1 * lines[0:1, :]).astype(BF16)
+    loads["wa"].wait()
+    loads["probs"].wait()
+    other_b = d_resid_b.at[at.twin]
+    landed(other_b, ysems.at[0], yrecv.at[0], tensor=at.twin)
+
+    d_attn[...] = jnp.dot(
+        d_resid_b[...].reshape(rows, width), wa[:, qkv_cols:qkv_cols + q_cols],
+        preferred_element_type=F32,
+    ).astype(BF16)
+    rets[2].over_s()
+    cos_t, sin_t = cosine[...], sine[...]
+
+    def unrotated(values):
+        return values * cos_t - pltpu.roll(values, HD // 2, 1) * sin_t
+
+    bias_rows = [None] * (heads + 2 * kv)
+
+    def place(head, grad):
+        bias_rows[head] = jnp.sum(grad, axis=0, keepdims=True)
+        d_projb[:, head * HD:(head + 1) * HD] = grad.astype(BF16)
+
+    repeat = heads // kv
+    for j in range(kv):
+        keys = kv_all[:, :, j * HD:(j + 1) * HD].reshape(group_rows, HD)
+        values = kv_all[:, :, (kv + j) * HD:(kv + j + 1) * HD].reshape(group_rows, HD)
+        d_values = jnp.zeros((group_rows, HD), F32)
+        d_keys = jnp.zeros((group_rows, HD), F32)
+        for h in range(j * repeat, (j + 1) * repeat):
+            d_out = d_attn[:, h * HD:(h + 1) * HD]
+            p = probs[h * rows:(h + 1) * rows, :]
+            d_prob = turn_last(d_out, values)
+            delta = jnp.sum(
+                d_out.astype(F32) * attn[:, h * HD:(h + 1) * HD].astype(F32), axis=1, keepdims=True
+            )
+            d_s = (p * (d_prob - delta)).astype(BF16)
+            d_score[...] = d_s
+            place(h, unrotated(jnp.dot(d_s, keys, preferred_element_type=F32) * scale))
+            d_keys = d_keys + turn_first(d_score[...], query[:, h * HD:(h + 1) * HD])
+            d_values = d_values + turn_first(p.astype(BF16), d_out)
+        for i, grad in ((j, d_keys * scale), (kv + j, d_values)):
+            dkv[:, :, i * HD:(i + 1) * HD] = grad.astype(BF16).reshape(nz, rows, HD)
+    for d in range(1, nz):
+        sends.go(dkv.at[at.z_to(d)], dkv_land.at[d], dkvs.at[d], dkvr.at[d], context=at.z_to(d))
+    rets[0].over_z()
+    d_own = dkv[at.z].astype(F32)
+    for d in range(1, nz):
+        landed(dkv_land.at[d], dkvs.at[d], dkvr.at[d], context=at.z_from(d))
+        d_own = d_own + dkv_land[d].astype(F32)
+    for j in range(kv):
+        place(heads + j, unrotated(d_own[:, j * HD:(j + 1) * HD]))
+        place(heads + kv + j, d_own[:, (kv + j) * HD:(kv + j + 1) * HD])
+    dn1_part[...] = turn_last(d_projb[...], wa[:, :qkv_cols]).astype(BF16)
+    sends.go(dn1_part, dn1_land, ysems.at[2], yrecv.at[2], tensor=at.twin)
+    r_attn.give_all()
+    rets[1].over_z()
+    r_attn.over_s()
+
+    out_half = r_ffn.total() + resid[...]
+    block_out[at.y] = out_half.astype(BF16)
+    sends.go(block_out.at[at.y], block_out.at[at.y], ysems.at[3], yrecv.at[3], tensor=at.twin)
+
+    landed(dn1_land, ysems.at[2], yrecv.at[2], tensor=at.twin)
+    landed(d_resid_f.at[at.twin], ysems.at[1], yrecv.at[1], tensor=at.twin)
+    dn1 = dn1_part[...].astype(F32) + dn1_land[...].astype(F32)
+    hidden_f = hidden[...].astype(F32)
+    factor1 = lax.rsqrt(jnp.mean(hidden_f * hidden_f, axis=1, keepdims=True) + EPSILON)
+    unit1 = hidden_f * factor1
+    row = lax.broadcasted_iota(jnp.int32, (rows, 1), 0)
+    my_row = (row >= at.y * half) & (row < (at.y + 1) * half)
+    grad_g1 = jnp.sum(jnp.where(my_row, dn1 * unit1, 0.0), axis=0, keepdims=True)
+    scaled = dn1 * lines[0:1, :]
+    back1 = factor1 * (scaled - unit1 * jnp.mean(scaled * unit1, axis=1, keepdims=True))
+    input_grad[...] = d_resid_f[...].reshape(rows, width) + back1
+
+    gains = jnp.concatenate([grad_g1, grad_g2, jnp.zeros((6, width), F32)], axis=0)
+    bias = jnp.concatenate(bias_rows, axis=0)
+    each = HD // (ns * nz)
+    for b in range(ns * nz):
+        moved = pltpu.roll(bias, LANES - b * each, 1) if b else bias
+        small[b // nz, b % nz] = jnp.concatenate([piece_of_lines(gains, b, depth), moved], axis=0)
+    for k in range(1, ns):
+        s2 = lax.rem(at.s + k, ns)
+        sends.go(small.at[s2], small_land.at[k], shs.at[k], shr.at[k], shard=s2)
+    rets[2].over_z()
+    total = small[at.s]
+    for k in range(1, ns):
+        s1 = lax.rem(at.s - k + ns, ns)
+        landed(small_land.at[k], shs.at[k], shr.at[k], shard=s1)
+        total = total + small_land[k]
+    small_z[...] = total
+    for d in range(1, nz):
+        sends.go(small_z.at[at.z_to(d)], small_zland.at[d], szs.at[d], szr.at[d], context=at.z_to(d))
+    r_attn.over_z()
+    total = small_z[at.z]
+    for d in range(1, nz):
+        landed(small_zland.at[d], szs.at[d], szr.at[d], context=at.z_from(d))
+        total = total + small_zland[d]
+    small_y[...] = total
+    sends.go(small_y, small_yland, ysems.at[4], yrecv.at[4], tensor=at.twin)
+    for ret in rets:
+        ret.finish()
+    landed(small_yland, ysems.at[4], yrecv.at[4], tensor=at.twin)
+    small_out[:8, :] = small_y[:8, :] + small_yland[:8, :]
+    small_out[8:, :] = small_y[8:, :]
+    landed(block_out.at[at.twin], ysems.at[3], yrecv.at[3], tensor=at.twin)
+    r_attn.finish()
+    total = attn_land[0].astype(F32)
+    for z1 in range(1, nz):
+        total = total + attn_land[z1].astype(F32)
+    attn_grad[...] = total
+    sends.drain()
+
+
+def back(ns, nz, heads, kv, wa, n2, cot, act, d_gate, d_up, probs, dn2_part, ffn_part, hidden, resid,
+         cot_own, lines, query, kv_all, attn, cosine, sine):
+    rows, width = hidden.shape
+    owners, half, group_rows = ns * nz, rows // 2, nz * rows
+    depth, unit = width // owners, act.shape[1]
+    q_cols = heads * HD
+    cols = wa.shape[1]
+    dma = pltpu.SemaphoreType.DMA
+    shape = jax.ShapeDtypeStruct
+    vmem = pl.BlockSpec(memory_space=pltpu.VMEM)
+    anyspace = pl.BlockSpec(memory_space=pl.ANY)
+    parts = (nz, 2, half, width)
+    big = (wa, n2, cot, act, d_gate, d_up, probs)
+    scratch = [pltpu.VMEM(a.shape, a.dtype) for a in big] + [dma((len(big),))]
+    for _ in range(3):
+        scratch += Return.bufs(ns, nz, depth, unit) + Return.sems(ns, nz)
+    scratch += Return.bufs(ns, nz, depth, cols) + Return.sems(ns, nz)
+    scratch += [
+        pltpu.VMEM((nz, depth, cols), BF16),
+        pltpu.VMEM((rows, width), BF16),
+        pltpu.VMEM((2, half, width), BF16),
+        pltpu.VMEM((rows, cols - q_cols), BF16),
+    ]
+    for _ in range(2):
+        scratch += Reduce.bufs(nz, half, width) + Reduce.sems(nz)
+    scratch += [
+        pltpu.VMEM((2, half, width), F32),
+        pltpu.VMEM((rows, q_cols), BF16),
+        pltpu.VMEM((rows, group_rows), BF16),
+        pltpu.VMEM((nz, rows, 2 * kv * HD), BF16),
+        pltpu.VMEM((nz, rows, 2 * kv * HD), BF16),
+        pltpu.VMEM((rows, width), BF16),
+        pltpu.VMEM((rows, width), BF16),
+        pltpu.VMEM((ns, nz, 16, LANES), F32),
+        pltpu.VMEM((ns, nz, 16, LANES), F32),
+        pltpu.VMEM((nz, 16, LANES), F32),
+        pltpu.VMEM((nz, 16, LANES), F32),
+        pltpu.VMEM((16, LANES), F32),
+        pltpu.VMEM((16, LANES), F32),
+        dma((nz,)), dma((nz,)), dma((ns,)), dma((ns,)), dma((nz,)), dma((nz,)), dma((5,)), dma((5,)),
+    ]
+    return pl.pallas_call(
+        functools.partial(back_kernel, ns, nz, heads, kv),
+        out_shape=[
+            shape((2, half, width), BF16),
+            shape((rows, width), F32),
+            shape((depth, cols), F32),
+            shape((16, LANES), F32),
+            *[shape((nz, depth, unit), BF16)] * 3,
+        ],
+        in_specs=[anyspace] * 7 + [vmem] * 11,
+        out_specs=[vmem] * 4 + [anyspace] * 3,
+        scratch_shapes=scratch,
+        compiler_params=pltpu.CompilerParams(
+            collective_id=1, has_side_effects=True, vmem_limit_bytes=VMEM_BYTES
+        ),
+    )(*big, dn2_part.reshape(parts), ffn_part.reshape(parts), hidden, resid, cot_own, lines, query,
+      kv_all, attn, cosine, sine)
+
+
 def fast_step(
     ns,
     nz,
@@ -455,11 +917,7 @@
     parts = 2
     heads = H // parts
     kv = KVH // parts
-    repeat = heads // kv
-    scale = HD ** (-0.5)
     block_index = lax.axis_index("context")
-    part_index = lax.axis_index("tensor")
-    half_rows = rows // parts
     unit_cols = -(-hidden_units // (nz * LANES)) * LANES
     padded = unit_cols * nz
     q_cols = heads * HD
@@ -491,94 +949,30 @@
         ns, nz, heads, kv, wa_in, small_in, ffn_in, hidden_in, out_cotangent, cosine, sine,
         allowed.astype(F32),
     )
-    gain_one, gain_two = lines[0], lines[1]
-    qkv_full = wa[:, : q_cols + 2 * k_cols]
-    out_full = wa[:, q_cols + 2 * k_cols :]
-    normed2 = n2.reshape(group_rows, width)
-    cot = cot.reshape(group_rows, width)
-    hidden_f = hidden_in.astype(F32)
-    normed1, unit1, factor1 = norm_forward(hidden_f, gain_one)
-    _, unit2, factor2 = norm_forward(resid_half, gain_two)
-    query = jnp.transpose(query.reshape(rows, heads, HD), (1, 0, 2)).reshape(kv, repeat * rows, HD)
-    kv_rows = kv_all.reshape(group_rows, 2 * kv, HD)
-    keys = jnp.transpose(kv_rows[:, :kv], (1, 0, 2))
-    values = jnp.transpose(kv_rows[:, kv:], (1, 0, 2))
-    p_soft = p_soft.reshape(kv, repeat * rows, group_rows)
-    probs = p_soft.astype(BF16)
-    outs = jnp.transpose(attn.reshape(rows, heads, HD), (1, 0, 2)).reshape(kv, repeat * rows, HD)
-    mine = part_index * half_rows
-    cot_half = lax.dynamic_slice_in_dim(out_cotangent, mine, half_rows)
-    blocks = nz
-    gate = dot(normed2, gate_full)
-    up_val = dot(normed2, up_full)
-    sigma = jax.nn.sigmoid(gate)
-    silu_val = gate * sigma
-    act = (silu_val * up_val).astype(BF16)
-    ffn_part = contract_last(act, down_full).astype(BF16)
-    d_act = dot(cot, down_full)
-    d_gate = (d_act * up_val * sigma * (1.0 + gate * (1.0 - sigma))).astype(BF16)
-    d_up = (d_act * silu_val).astype(BF16)
-    dn2_part = (contract_last(d_gate, gate_full) + contract_last(d_up, up_full)).astype(BF16)
-    ffn_half = lax.psum_scatter(ffn_part, TEAM, scatter_dimension=0, tiled=True)
-    block_half = (resid_half + ffn_half.astype(F32)).astype(BF16)
-    block_out = lax.all_gather(block_half, "tensor", axis=0, tiled=True)
-    dn2_half = lax.psum_scatter(dn2_part, TEAM, scatter_dimension=0, tiled=True).astype(F32)
-    grad_g2, d_back2 = norm_backward(dn2_half, unit2, factor2, gain_two)
-    d_resid_half = cot_half.astype(F32) + d_back2
-
-    def give_back(grad):
-        part = lax.psum_scatter(grad.astype(BF16), "shard", scatter_dimension=0, tiled=True)
-        part = part.reshape(blocks, depth, unit_cols)
-        part = lax.all_to_all(part, "context", split_axis=0, concat_axis=2, tiled=True)
-        return part.reshape(depth, padded)[:, :hidden_units].astype(F32)
-
-    sum_gate = give_back(contract_first(normed2, d_gate))
-    sum_up = give_back(contract_first(normed2, d_up))
-    sum_down = give_back(contract_first(cot, act)).T
-
-    d_resid_b = lax.all_gather(d_resid_half.astype(BF16), "tensor", axis=0, tiled=True)
-    grad_out = contract_first(d_resid_b, attn)
-    d_attn = dot(d_resid_b, out_full).astype(BF16)
-    d_outs = jnp.transpose(d_attn.reshape(rows, heads, HD), (1, 0, 2)).reshape(
-        kv, repeat * rows, HD
-    )
-    d_prob = batched(d_outs, values, 2, 2)
-    delta = jnp.sum(d_outs.astype(F32) * outs.astype(F32), axis=2, keepdims=True)
-    d_score = (p_soft * (d_prob - delta)).astype(BF16)
-    d_query = batched(d_score, keys, 2, 1) * scale
-    d_keys = batched(d_score, query, 1, 1) * scale
-    d_values = batched(probs, d_outs, 1, 1)
-    d_kv = jnp.concatenate([d_keys, d_values], axis=0).astype(BF16)
-    d_kv = lax.psum_scatter(d_kv, "context", scatter_dimension=1, tiled=True).astype(F32)
-    d_query = unrotate(d_query.reshape(heads, rows, HD), cosine, sine)
-    d_keys = unrotate(d_kv[:kv], cosine, sine)
-    d_proj = jnp.transpose(jnp.concatenate([d_query, d_keys, d_kv[kv:]], axis=0), (1, 0, 2))
-    grad_bias = jnp.sum(d_proj, axis=0)
-    d_projb = d_proj.reshape(rows, -1).astype(BF16)
-    grad_qkv = contract_first(normed1, d_projb)
-    dn1_part = contract_last(d_projb, qkv_full).astype(BF16)
-    dn1_half = lax.psum_scatter(dn1_part, "tensor", scatter_dimension=0, tiled=True).astype(F32)
-    unit1_half = lax.dynamic_slice_in_dim(unit1, mine, half_rows)
-    factor1_half = lax.dynamic_slice_in_dim(factor1, mine, half_rows)
-    grad_g1, d_back1 = norm_backward(dn1_half, unit1_half, factor1_half, gain_one)
-    input_grad = lax.all_gather(d_resid_half + d_back1, "tensor", axis=0, tiled=True)
-
-    gains = lax.psum(jnp.stack([grad_g1, grad_g2]), "tensor")
-    sum_gains = lax.psum_scatter(gains, OWNERS, scatter_dimension=1, tiled=True)
-    sum_qkv = lax.psum_scatter(grad_qkv.astype(BF16), OWNERS, scatter_dimension=0, tiled=True)
-    sum_bias = lax.psum_scatter(grad_bias, OWNERS, scatter_dimension=1, tiled=True)
-    sum_out = lax.psum_scatter(grad_out.astype(BF16), OWNERS, scatter_dimension=0, tiled=True)
+    act, d_gate, d_up, ffn_part, dn2_part = ffn(
+        gate_full, up_full, down_full, n2.reshape(group_rows, width), cot.reshape(group_rows, width)
+    )
+    block_out, input_grad, attn_grad, small, grad_gate, grad_up, grad_down = back(
+        ns, nz, heads, kv, wa, n2.reshape(group_rows, width), cot.reshape(group_rows, width), act,
+        d_gate, d_up, p_soft, dn2_part, ffn_part, hidden_in, resid_half, out_cotangent, lines, query,
+        kv_all, attn, cosine, sine,
+    )
+
+    def all_columns(grad):
+        return jnp.transpose(grad, (1, 0, 2)).reshape(depth, padded)[:, :hidden_units].astype(F32)
+
+    qkv_cols = q_cols + 2 * k_cols
     return (
-        block_out,
+        block_out.reshape(rows, width),
         input_grad,
-        sum_gains[0],
-        sum_qkv.astype(F32),
-        sum_bias,
-        sum_out.astype(F32).T,
-        sum_gains[1],
-        sum_gate,
-        sum_up,
-        sum_down,
+        small[0, :depth],
+        attn_grad[:, :qkv_cols],
+        small[8:, : qkv_bias.shape[1]],
+        attn_grad[:, qkv_cols:].T,
+        small[1, :depth],
+        all_columns(grad_gate),
+        all_columns(grad_up),
+        all_columns(grad_down).T,
     )
 
 

time: 756 us -> 361 us (0.48)
  waiting for transfers between devices: 399 us -> 0 us
  Pallas kernels: 157 us -> 336 us
  blocking collectives: 66.8 us -> 0 us
  matrix products: 53.4 us -> 0 us
  starting transfers between devices: 17.8 us -> 0 us
  between operations: 15.5 us -> 0.78 us
  other arithmetic: 21.4 us -> 11.7 us
    reduce_scatter x9 -> x0, waiting for transfers between devices: 340 us -> none  [the longest x1 68.1 us: fast_step(): lax.psum_scatter(dn2_part, TEAM, scatter_dimension=0, tiled=True)]
    pallas_call x0 -> x2, Pallas kernels: none -> 180 us  [the longest x1 157 us: back(): pl.pallas_call(functools.partial(back_kernel, ns, nz, heads, kv), out_sha...]
    dot_general x17 -> x0, matrix products: 53.4 us -> none  [the longest x5 22.4 us: contract_first(): lax.dot_general(left, right, (((0,), (0,)), ((), ())), preferred_element_...]
    unnamed x11 -> x0, waiting for transfers between devices: 44.1 us -> none
    unnamed x1 -> x0, blocking collectives: 40.6 us -> none
    all_gather x3 -> x0, blocking collectives: 21.2 us -> none  [the longest x1 8.43 us: fast_step(): lax.all_gather(d_resid_half + d_back1, 'tensor', axis=0, tiled=True)]
    all_to_all x3 -> x0, starting transfers between devices: 17.2 us -> none  [give_back(): lax.all_to_all(part, 'context', split_axis=0, concat_axis=2, tiled=True)]
    all_to_all x3 -> x0, waiting for transfers between devices: 15.6 us -> none  [give_back(): lax.all_to_all(part, 'context', split_axis=0, concat_axis=2, tiled=True)]
  transfers between devices with their start and end apart: 13 -> 0, of which waited for: 9 -> 0; matrix products, arithmetic and copies ran while one was open for 7% -> 0% of each run, Pallas kernels for 0% -> 0%
where the time goes in v2:
time: 361 us
  Pallas kernels  336 us (93%)
  local copies, waits for them, and re-layouts  12.1 us (3%)
  other arithmetic  11.7 us (3%)
    pallas_call x1, Pallas kernels, back(): pl.pallas_call(functools.partial(back_kernel, ns, nz, heads, kv), out_sha...  157 us
    pallas_call x1, Pallas kernels, front(): pl.pallas_call(functools.partial(front_kernel, ns, nz, heads, kv), out_sh...  157 us
    pallas_call x1, Pallas kernels, ffn(): pl.pallas_call(ffn_kernel, out_shape=[shape((rows, unit), BF16)] * 3 + [s...  22.1 us

profile of v2, /device:TPU:10, one launch (start us, length us, event | category | flops | bytes accessed | tf_op | source)
XLA Modules:
  0.0 360.7 jit_solution(13721857930182166666)
XLA Ops:
  0.6 0.0 copy-start.3
  0.7 0.7 dynamic-slice_bitcast_fusion
  1.4 0.9 convert_reduce_fusion
  2.3 0.7 fusion.10
  3.0 1.3 fusion.4.refs_1_
  4.2 0.3 fusion.2
  4.6 0.7 pad_maximum_fusion.2.refs_8_.refs_17_
  5.3 0.7 pad_maximum_fusion.1.refs_7_.refs_16_
  6.0 1.5 fusion.1.refs_9_
  7.5 1.8 pad_maximum_fusion.refs_0_
  9.2 0.0 copy-done.3
  9.2 0.0 copy-start.4
  9.2 0.1 pad.20
  9.3 0.0 copy-start.5
  9.3 1.0 copy.36
  10.3 0.3 copy-done.4
  10.6 0.1 pad.21
  10.7 0.3 copy-done.5
  11.0 0.1 pad.22
  11.1 1.3 bitcast_bitcast_fusion
  12.4 156.6 %shard_map.186 = (bf16[1536,1792]{1,0:T(8,128)(2,1)}, bf16[1536,1152]{1,0:T(8,128)(2,1)}, bf16[1536,1152]{1,0:T(8,128)(2,1)}, bf16[1536,1152]{1,0:T(8,128)(2,1)}...) custom-call(bf16[96,1792]{1,0:T(8,128)(2,1)} %pad_maximum_fusion.ref, ...), custom_call_target="tpu_custom_call" | custom-call | tf_op jit(solution)/shard_map/pallas_call | solution.py:414
  169.0 22.1 %shard_map.187 = (bf16[512,1152]{1,0:T(8,128)(2,1)}, bf16[512,1152]{1,0:T(8,128)(2,1)}, bf16[512,1152]{1,0:T(8,128)(2,1)}, bf16[512,1536]{1,0:T(8,128)(2,1)}, bf16[512,1536]{1,0:T(8,128)(2,1)}) custom-call(bf16[1536,1152]{1,0:T(8,128)(2,1)} %get-tuple-element.37.gate_in, bf16[1536,1152]{1,0:T(8,128)(2,1)} %get-tuple-element.38.up_in, ...), custom_call_target="tpu_custom_call" | custom-call | tf_op jit(solution)/shard_map/pallas_call | solution.py:483
  191.1 157.4 %shard_map.188 = (bf16[2,64,1536]{2,1,0:T(8,128)(2,1)}, f32[128,1536]{1,0:T(8,128)}, f32[96,1792]{1,0:T(8,128)}, f32[16,128]{1,0:T(8,128)}, bf16[4,96,1152]{2,1,...) custom-call(bf16[1536,1792]{1,0:T(8,128)(2,1)} %get-tuple-element.34.refs_0_, ...), custom_call_target="tpu_custom_call" | custom-call | tf_op jit(solution)/shard_map/pallas_call | solution.py:881
  348.6 0.0 copy-start.2
  348.6 1.3 slice_bitcast_fusion.1
  349.8 1.3 slice.26
  351.1 1.7 slice_bitcast_fusion
  352.8 1.8 slice.25
  354.6 0.0 copy-done.2
  354.6 0.1 copy.30
  354.6 0.0 copy-start.1
  354.7 1.3 slice_convert_fusion.1
  356.0 0.2 copy-done.1
  356.1 0.1 copy.31
  356.2 0.0 copy-start
  356.2 1.3 slice_convert_fusion
  357.5 0.2 copy-done
  357.7 0.1 copy.32
  357.7 0.0 copy-start.7
  357.8 0.0 copy-start.6
  357.8 1.3 convert_bitcast_fusion
  359.1 0.0 copy-done.7
  359.1 0.7 copy.39
  359.8 0.0 copy-done.6
  359.8 0.9 copy.40
  (2 shorter events, 0.0 us)
Async XLA Ops:
  0.6 8.6 %copy-start.3 = (bf16[96,4480]{1,0:T(8,128)(2,1)S(1)}, bf16[96,4480]{1,0:T(8,128)(2,1)}, u32[]{:S(2)}) copy-start(bf16[96,4480]{1,0:T(8,128)(2,1)} %param.18) | copy-start | bytes 2580484
  9.2 1.4 copy-start.4
  9.3 1.7 copy-start.5
  348.6 6.0 %copy-start.2 = (bf16[4,96,1152]{2,1,0:T(8,128)(2,1)S(1)}, bf16[4,96,1152]{2,1,0:T(8,128)(2,1)}, u32[]{:S(2)}) copy-start(bf16[4,96,1152]{2,1,0:T(8,128)(2,1)} %get-tuple-element.55) | copy-start | bytes 2654212
  354.6 1.5 copy-start.1
  356.2 1.5 copy-start
  357.7 1.3 copy-start.7
  357.8 2.1 copy-start.6

commit v3 on v1

--- a/solution.py
+++ b/solution.py
@@ -102,11 +102,17 @@
     def mate_from(self, o):
         return lax.rem(self.outer - o + self.no, self.no) * 2 + 1 - self.core
 
-    def greet(self):
+    def mate_to(self, o):
+        return lax.rem(self.outer + o, self.no) * 2 + 1 - self.core
+
+    def greet(self, everyone=False):
         barrier = pltpu.get_barrier_semaphore()
         peers = [{"context": self.z_to(d)} for d in range(1, self.nz)]
-        peers += [{"shard": self.s_to(o)} for o in range(1, self.no)]
-        peers += [{"shard": self.mate}, {"tensor": self.twin}]
+        if everyone:
+            peers += [{"shard": lax.rem(self.s + k, self.ns)} for k in range(1, self.ns)]
+        else:
+            peers += [{"shard": self.s_to(o)} for o in range(1, self.no)] + [{"shard": self.mate}]
+        peers += [{"tensor": self.twin}]
         for peer in peers:
             pl.semaphore_signal(barrier, inc=1, device_id=peer, device_id_type=MESH)
         pl.semaphore_wait(barrier, len(peers))
@@ -116,13 +122,13 @@
     def __init__(self):
         self.remote, self.local = [], []
 
-    def go(self, src, dst, send, recv, **peer):
+    def go(self, src, dst, send, recv, only=None, **peer):
         copy = pltpu.make_async_remote_copy(
             src_ref=src, dst_ref=dst, send_sem=send, recv_sem=recv,
             device_id=peer, device_id_type=MESH,
         )
-        copy.start()
-        self.remote.append(copy)
+        guarded(only, copy.start)
+        self.remote.append((only, copy.wait_send))
 
     def here(self, src, dst, sem):
         copy = pltpu.make_async_copy(src, dst, sem)
@@ -130,118 +136,240 @@
         self.local.append(copy)
 
     def drain(self):
-        for copy in self.remote:
-            copy.wait_send()
+        for only, wait in self.remote:
+            guarded(only, wait)
         for copy in self.local:
             copy.wait()
         self.remote, self.local = [], []
 
 
-def landed(ref, send, recv, **peer):
-    pltpu.make_async_remote_copy(
+def guarded(only, action):
+    if only is None:
+        action()
+    else:
+        pl.when(only)(action)
+
+
+def landed(ref, send, recv, only=None, **peer):
+    copy = pltpu.make_async_remote_copy(
         src_ref=ref, dst_ref=ref, send_sem=send, recv_sem=recv,
         device_id=peer, device_id_type=MESH,
-    ).wait_recv()
+    )
+    guarded(only, copy.wait_recv)
+
+
+def far_first(n):
+    return [n - 1 - i // 2 if i % 2 == 0 else i // 2 for i in range(n)]
+
+
+class Chain:
+    def __init__(self, at, sends, ref, sems):
+        self.at, self.sends, self.ref = at, sends, ref
+        self.zs, self.zr = sems
+
+    @staticmethod
+    def sems(nz):
+        dma = pltpu.SemaphoreType.DMA
+        return [dma((2, nz)), dma((nz,))]
+
+    def hops(self, steps=None):
+        at = self.at
+        for k in steps or range(1, at.nz):
+            yield (-1, at.z - k >= 0, at.z - k)
+            yield (1, at.z + k < at.nz, at.z + k)
+
+    def hand(self, way, origin, src, only):
+        at = self.at
+        there = at.z + 1 < at.nz if way == 0 else at.z > 0
+        self.sends.go(
+            src, self.ref(origin), self.zs.at[way, origin], self.zr.at[origin],
+            only=there if only is None else there & only, context=at.z + (1 if way == 0 else -1),
+        )
+
+    def begin(self, src):
+        for way in range(2):
+            self.hand(way, self.at.z, src, None)
+
+    def step(self, side, valid, origin):
+        ref = self.ref(origin)
+        landed(ref, self.zs.at[0, origin], self.zr.at[origin], only=valid, context=self.at.z)
+        self.hand(0 if side < 0 else 1, origin, ref, valid)
+        return ref
+
+
+class ChainSum:
+    def __init__(self, at, sends, bufs, sems):
+        self.at, self.sends = at, sends
+        stage, self.land = bufs
+        self.stage = stage if callable(stage) else lambda z2: stage.at[z2]
+        self.zs, self.zr = sems
+
+    @staticmethod
+    def sems(nz):
+        dma = pltpu.SemaphoreType.DMA
+        return [dma((nz,)), dma((nz + 1,))]
+
+    @staticmethod
+    def bufs(nz, shape, dtype=BF16):
+        return [pltpu.VMEM((nz, *shape), dtype), pltpu.VMEM((nz + 1, *shape), dtype)]
+
+    def put(self, z2, own):
+        at = self.at
+        stage, dtype = self.stage(z2), self.land.dtype
+
+        def start(slot, before):
+            slot_ref = self.land.at[z2]
+
+            @pl.when(before)
+            def _():
+                landed(slot_ref, self.zs.at[z2], self.zr.at[z2], context=at.z)
+                stage[...] = (own() + self.land[z2].astype(F32)).astype(dtype)
+
+            @pl.when(jnp.logical_not(before))
+            def _():
+                stage[...] = own().astype(dtype)
+
+            pltpu.make_async_remote_copy(
+                src_ref=stage, dst_ref=self.land.at[slot], send_sem=self.zs.at[z2],
+                recv_sem=self.zr.at[slot], device_id={"context": at.z + (1 if z2_right else -1)},
+                device_id_type=MESH,
+            ).start()
+
+        for z2_right in (True, False):
+            away = at.z < z2 if z2_right else at.z > z2
+
+            @pl.when(away)
+            def _(z2_right=z2_right):
+                near = at.z + 1 == z2 if z2_right else at.z - 1 == z2
+                slot = z2 if z2_right else z2 + near * (at.nz - z2)
+                before = at.z > 0 if z2_right else at.z + 1 < at.nz
+                start(slot, before)
+
+        self.sends.remote.append((
+            at.z != z2,
+            lambda: pltpu.make_async_remote_copy(
+                src_ref=stage, dst_ref=self.land.at[z2], send_sem=self.zs.at[z2],
+                recv_sem=self.zr.at[z2], device_id={"context": at.z}, device_id_type=MESH,
+            ).wait_send(),
+        ))
+
+    def total(self, own):
+        at = self.at
+        total = own
+        for slot, there in ((at.z, at.z > 0), (at.nz, at.z + 1 < at.nz)):
+            landed(self.land.at[slot], self.zs.at[0], self.zr.at[slot], only=there, context=at.z)
+            total = total + jnp.where(there, self.land[slot].astype(F32), 0.0)
+        return total
 
 
 class Spread:
-    def __init__(self, at, sends, src, dst, sems):
+    def __init__(self, at, sends, src, dst, sems, same=False):
         self.at, self.sends, self.src, self.dst = at, sends, src, dst
         self.copy = None
-        self.own, self.zs, self.zr, self.xs, self.xr, self.cs, self.cr = sems
+        self.own, self.zs, self.zr, self.xs, self.xr, self.cs, self.cr, *chain = sems
+        self.chain = Chain(at, sends, lambda z1: dst(at.s, z1), chain) if same else None
 
     @staticmethod
     def sems(ns, nz):
         dma, no = pltpu.SemaphoreType.DMA, ns // 2
         return [
             dma, dma((nz,)), dma((nz,)), dma((nz, no)), dma((nz, no)), dma((no, nz)), dma((no, nz)),
-        ]
+        ] + Chain.sems(nz)
 
     def over_z(self):
         at = self.at
+        if self.chain is not None:
+            self.chain.begin(self.src(at.z))
+            return
         for d in range(1, at.nz):
             z2 = at.z_to(d)
-            self.sends.go(self.src(z2), self.dst(at.s, at.z), self.zs.at[d], self.zr.at[d], context=z2)
-
-    def over_s(self, d, ref):
+            self.sends.go(
+                self.src(z2), self.dst(at.s, at.z), self.zs.at[z2], self.zr.at[at.z], context=z2
+            )
+
+    def over_s(self, z1, ref, only=None):
         at = self.at
         for o in range(1, at.no):
             self.sends.go(
-                ref, self.dst(at.s, at.z_from(d)), self.xs.at[d, o], self.xr.at[d, o],
+                ref, self.dst(at.s, z1), self.xs.at[z1, o], self.xr.at[z1, o], only=only,
                 shard=at.s_to(o),
             )
         self.sends.go(
-            ref, self.dst(at.s, at.z_from(d)), self.cs.at[0, d], self.cr.at[0, d], shard=at.mate
+            ref, self.dst(at.s, z1), self.cs.at[0, z1], self.cr.at[0, z1], only=only, shard=at.mate
         )
 
     def own_block(self):
         at = self.at
-        self.over_s(0, self.src(at.z))
+        self.over_s(at.z, self.src(at.z))
         self.copy = pltpu.make_async_copy(self.src(at.z), self.dst(at.s, at.z), self.own)
         self.copy.start()
 
-    def pass_z(self, d):
-        at = self.at
-        ref = self.dst(at.s, at.z_from(d))
-        landed(ref, self.zs.at[d], self.zr.at[d], context=at.z_from(d))
-        self.over_s(d, ref)
-
-    def pass_s(self, o, d):
-        at = self.at
-        s1 = at.s_from(o)
-        ref = self.dst(s1, at.z_from(d))
-        landed(ref, self.xs.at[d, o], self.xr.at[d, o], shard=s1)
-        self.sends.go(ref, ref, self.cs.at[o, d], self.cr.at[o, d], shard=at.mate)
+    def pass_z(self):
+        at = self.at
+        if self.chain is not None:
+            for side, valid, z1 in self.chain.hops():
+                self.over_s(z1, self.chain.step(side, valid, z1), only=valid)
+            return
+        for d in range(1, at.nz):
+            z1 = at.z_from(d)
+            ref = self.dst(at.s, z1)
+            landed(ref, self.zs.at[z1], self.zr.at[z1], context=z1)
+            self.over_s(z1, ref)
+
+    def pass_s(self):
+        at = self.at
+        for o in range(1, at.no):
+            s1 = at.s_from(o)
+            for d in range(at.nz):
+                z1 = at.z_from(d)
+                ref = self.dst(s1, z1)
+                landed(ref, self.xs.at[z1, o], self.xr.at[z1, o], shard=s1)
+                self.sends.go(ref, ref, self.cs.at[o, z1], self.cr.at[o, z1], shard=at.mate)
 
     def finish(self):
         at = self.at
         self.copy.wait()
         for o in range(at.no):
-            for d in range(at.nz):
-                ref = self.dst(at.mate_from(o), at.z_from(d))
-                landed(ref, self.cs.at[o, d], self.cr.at[o, d], shard=at.mate)
+            for z1 in range(at.nz):
+                ref = self.dst(at.mate_from(o), z1)
+                landed(ref, self.cs.at[o, z1], self.cr.at[o, z1], shard=at.mate)
 
     def pass_all(self):
-        for d in range(1, self.at.nz):
-            self.pass_z(d)
-        for o in range(1, self.at.no):
-            for d in range(self.at.nz):
-                self.pass_s(o, d)
+        self.pass_z()
+        self.pass_s()
 
 
 class Tokens:
     def __init__(self, at, sends, ref, sems):
         self.at, self.sends, self.ref = at, sends, ref
-        self.zs, self.zr, self.ys, self.yr = sems
+        self.ys, self.yr, *chain = sems
+        self.chain = Chain(at, sends, lambda z1: ref.at[z1, at.y], chain)
 
     @staticmethod
     def sems(nz):
         dma = pltpu.SemaphoreType.DMA
-        return [dma((nz,)), dma((nz,)), dma((nz,)), dma((nz,))]
+        return [dma((nz,)), dma((nz,))] + Chain.sems(nz)
 
     def over_z(self, src):
-        at = self.at
-        for d in range(1, at.nz):
-            self.sends.go(
-                src, self.ref.at[at.z, at.y], self.zs.at[d], self.zr.at[d], context=at.z_to(d)
+        self.chain.begin(src)
+
+    def over_y(self, z1, src, only=None):
+        at = self.at
+        self.sends.go(
+            src, self.ref.at[z1, at.y], self.ys.at[z1], self.yr.at[z1], only=only, tensor=at.twin
+        )
+
+    def pass_z(self, steps=None):
+        for side, valid, z1 in self.chain.hops(steps):
+            self.over_y(z1, self.chain.step(side, valid, z1), only=valid)
+
+    def wait_y(self, places, only=None):
+        at = self.at
+        for z1 in places:
+            ref = self.ref.at[z1, at.twin]
+            landed(
+                ref, self.ys.at[z1], self.yr.at[z1], only=only and only(z1), tensor=at.twin
             )
-
-    def over_y(self, d, src):
-        at = self.at
-        self.sends.go(
-            src, self.ref.at[at.z_from(d), at.y], self.ys.at[d], self.yr.at[d], tensor=at.twin
-        )
-
-    def pass_z(self, d):
-        at = self.at
-        ref = self.ref.at[at.z_from(d), at.y]
-        landed(ref, self.zs.at[d], self.zr.at[d], context=at.z_from(d))
-        self.over_y(d, ref)
-
-    def wait_y(self, d):
-        at = self.at
-        ref = self.ref.at[at.z_from(d), at.twin]
-        landed(ref, self.ys.at[d], self.yr.at[d], tensor=at.twin)
 
 
 def whole_lines(small, blocks, depth):
@@ -258,57 +386,262 @@
     return jnp.concatenate(tiles, axis=1)
 
 
-def front_kernel(ns, nz, heads, kv, *refs):
-    ins, outs, (small, ypart, yland, *sems) = refs[:10], refs[10:22], refs[22:]
-    (wa_in, small_in, gate_in, up_in, down_in, hidden, cot_in, cosine, sine, mask) = ins
-    (wa, gate_w, up_w, down_w, lines, n2, cot, resid, query, kv_all, probs, attn) = outs
-    n_spread = len(Spread.sems(ns, nz))
-    n_tokens = len(Tokens.sems(nz))
-    at, sends = Place(ns, nz), Sends()
+def turn_first(left, right):
+    return lax.dot_general(left, right, (((0,), (0,)), ((), ())), preferred_element_type=F32)
+
+
+def turn_last(left, right):
+    return lax.dot_general(left, right, (((1,), (1,)), ((), ())), preferred_element_type=F32)
+
+
+class Return:
+    def __init__(self, at, sends, make, room, lands, out, sems):
+        self.at, self.sends, self.make, self.out = at, sends, make, out
+        self.stage, self.acc = room.at[pl.ds(0, at.no)], room.at[pl.ds(at.no, at.no)]
+        self.landc, self.landx = lands
+        self.cs, self.cr, self.xs, self.xr, self.zs, self.zr, self.own = sems
+        self.chain = None
+        self.depth = self.acc.shape[1] // at.nz
+        self.copy = None
+
+    @staticmethod
+    def sems(ns, nz):
+        dma, no = pltpu.SemaphoreType.DMA, ns // 2
+        return [
+            dma((no,)), dma((no,)), dma((no, nz)), dma((no, nz)), dma((nz,)), dma((nz,)), dma,
+        ]
+
+    @staticmethod
+    def lands(ns, nz, depth, cols):
+        no = ns // 2
+        return [pltpu.VMEM((n, nz * depth, cols), BF16) for n in (no, no - 1)]
+
+    def give(self, o):
+        at = self.at
+        self.stage[o] = self.make(at.mate_to(o)).astype(BF16)
+        self.sends.go(
+            self.stage.at[o], self.landc.at[o], self.cs.at[o], self.cr.at[o], shard=at.mate
+        )
+        self.acc[o] = self.make(at.s_to(o)).astype(BF16)
+
+    def give_all(self):
+        for o in (*range(1, self.at.no), 0):
+            self.give(o)
+
+    def rows(self, z2):
+        start = z2 * self.depth
+        start = start if isinstance(start, int) else pl.multiple_of(start, SUBLANES)
+        return pl.ds(start, self.depth)
+
+    def piece(self, z2):
+        return self.acc.at[0, self.rows(z2)]
+
+    def order(self):
+        at = self.at
+        if self.chain is not None:
+            return far_first(at.nz)
+        return [at.z_to(d) for d in range(1, at.nz)] + [at.z]
+
+    def add(self, o, z2, others):
+        line = self.rows(z2)
+        total = self.acc[o, line, :].astype(F32)
+        for other, k in others:
+            total = total + other[k, line, :].astype(F32)
+        self.acc[o, line, :] = total.astype(BF16)
+
+    def over_s(self):
+        at = self.at
+        for o in range(1, at.no):
+            landed(self.landc.at[o], self.cs.at[o], self.cr.at[o], shard=at.mate)
+            for z2 in self.order():
+                self.add(o, z2, [(self.landc, o)])
+                line = self.rows(z2)
+                self.sends.go(
+                    self.acc.at[o, line], self.landx.at[o - 1, line], self.xs.at[o, z2],
+                    self.xr.at[o, z2], shard=at.s_to(o),
+                )
+        landed(self.landc.at[0], self.cs.at[0], self.cr.at[0], shard=at.mate)
+
+    def over_z(self, i):
+        at = self.at
+        z2 = self.order()[i]
+        line = self.rows(z2)
+        for o in range(1, at.no):
+            landed(self.landx.at[o - 1, line], self.xs.at[o, z2], self.xr.at[o, z2], shard=at.s_from(o))
+        self.add(0, z2, [(self.landc, 0)] + [(self.landx, o - 1) for o in range(1, at.no)])
+        if self.chain is not None:
+            self.chain.put(z2, lambda: self.piece(z2)[...].astype(F32))
+        elif i + 1 < at.nz:
+            self.sends.go(
+                self.piece(z2), self.out(at.z), self.zs.at[z2], self.zr.at[at.z], context=z2
+            )
+        else:
+            self.copy = pltpu.make_async_copy(self.piece(z2), self.out(z2), self.own)
+            self.copy.start()
+
+    def over_z_all(self):
+        for i in range(self.at.nz):
+            self.over_z(i)
+
+    def finish(self):
+        at = self.at
+        self.copy.wait()
+        for d in range(1, at.nz):
+            z1 = at.z_from(d)
+            landed(self.out(z1), self.zs.at[z1], self.zr.at[z1], context=z1)
+
+
+class Reduce:
+    def __init__(self, at, sends, parts, bufs, sems):
+        self.at, self.sends, self.parts = at, sends, parts
+        self.landy, *chain = bufs
+        self.ys, self.yr, *chain_sems = sems
+        self.chain = ChainSum(at, sends, chain, chain_sems)
+
+    @staticmethod
+    def sems(nz):
+        dma = pltpu.SemaphoreType.DMA
+        return [dma((nz,)), dma((nz,))] + ChainSum.sems(nz)
+
+    @staticmethod
+    def bufs(nz, half, width):
+        return [pltpu.VMEM((nz, half, width), BF16)] + ChainSum.bufs(nz, (half, width))
+
+    def over_y(self, places):
+        at = self.at
+        for z2 in places:
+            self.sends.go(
+                self.parts.at[z2, at.twin], self.landy.at[z2], self.ys.at[z2], self.yr.at[z2],
+                tensor=at.twin,
+            )
+
+    def own(self, z2):
+        return self.parts[z2, self.at.y].astype(F32) + self.landy[z2].astype(F32)
+
+    def pass_y(self):
+        at = self.at
+        for z2 in far_first(at.nz):
+            landed(self.landy.at[z2], self.ys.at[z2], self.yr.at[z2], tensor=at.twin)
+            self.chain.put(z2, lambda z2=z2: self.own(z2))
+
+    def total(self):
+        return self.chain.total(self.own(self.at.z))
+
+
+def piece_of_lines(lines, b, depth):
+    first, off = divmod(b * depth, LANES)
+    tile = lines[:, first * LANES:(first + 1) * LANES]
+    if not off:
+        return tile
+    tile = pltpu.roll(tile, LANES - off, 1)
+    if off + depth <= LANES:
+        return tile
+    after = pltpu.roll(lines[:, (first + 1) * LANES:(first + 2) * LANES], LANES - off, 1)
+    lane = lax.broadcasted_iota(jnp.int32, (8, LANES), 1)
+    return jnp.where(lane < LANES - off, tile, after)
+
+
+class Refs:
+    def __init__(self, refs):
+        self.refs, self.next = refs, 0
+
+    def take(self, n):
+        self.next += n
+        return self.refs[self.next - n:self.next]
+
+
+def layer_kernel(ns, nz, heads, kv, *refs):
+    refs = Refs(refs)
+    (wa_in, small_in, gate_in, up_in, down_in, hidden, cot_in, cosine, sine, mask) = refs.take(10)
+    (block_out, input_grad, qkv_grad, out_grad, small_out, *ffn_out) = refs.take(8)
+    at = Place(ns, nz)
+    w_sends, sends = Sends(), Sends()
     depth = wa_in.shape[0]
     rows, width = hidden.shape
     half = rows // 2
+    group_rows = nz * rows
     q_cols = heads * HD
     qkv_cols = q_cols + 2 * kv * HD
-
-    def spread(i, src, dst):
-        return Spread(at, sends, src, dst, sems[i * n_spread:(i + 1) * n_spread])
+    wide = nz * depth
+    scale = HD ** (-0.5)
+    repeat = heads // kv
+
+    wa, gate_w, up_w, down_w = refs.take(4)
+    n_spread, n_tokens, n_ret = len(Spread.sems(ns, nz)), len(Tokens.sems(nz)), len(Return.sems(ns, nz))
+    n_red, n_sum = len(Reduce.sems(nz)), len(ChainSum.sems(nz))
+    (small, ypart, yland, n2, cot, resid, query, kv_all, probs, attn) = refs.take(10)
 
     def block(ref):
-        return lambda s1, z1: ref.at[pl.ds(pl.multiple_of((s1 * nz + z1) * depth, SUBLANES), depth)]
-
-    w_attn = spread(0, lambda z2: wa_in, block(wa))
-    w_small = spread(1, lambda z2: small_in, lambda s1, z1: small.at[s1 * nz + z1])
+        return lambda s1, z1: ref.at[s1, pl.ds(pl.multiple_of(z1 * depth, SUBLANES), depth)]
+
+    w_attn = Spread(at, w_sends, lambda z2: wa_in, block(wa), refs.take(n_spread), True)
+    w_small = Spread(
+        at, w_sends, lambda z2: small_in, lambda s1, z1: small.at[s1 * nz + z1],
+        refs.take(n_spread), True,
+    )
     ffn = [
-        spread(2 + i, lambda z2, src=src: src.at[z2], block(dst))
-        for i, (src, dst) in enumerate(((gate_in, gate_w), (up_in, up_w), (down_in, down_w)))
+        Spread(at, w_sends, lambda z2, src=src: src.at[z2], block(dst), refs.take(n_spread))
+        for src, dst in ((gate_in, gate_w), (up_in, up_w), (down_in, down_w))
     ]
-    rest = sems[5 * n_spread:]
-    t_cot = Tokens(at, sends, cot, rest[:n_tokens])
-    t_n2 = Tokens(at, sends, n2, rest[n_tokens:2 * n_tokens])
-    kvs, kvr, yps, ypr, cot_sem = rest[2 * n_tokens:]
-
-    at.greet()
+    t_cot = Tokens(at, sends, cot, refs.take(n_tokens))
+    t_n2 = Tokens(at, sends, n2, refs.take(n_tokens))
+    kvs, kvr, yps, ypr, cot_sem = refs.take(5)
+    gate, up_val, d_act, act, d_gate, d_up, ffn_part, dn2_part = refs.take(8)
+    normed1_b, d_resid_b, d_projb = refs.take(3)
+
+    def columns(ref, s1):
+        return ref[..., pl.ds(pl.multiple_of(s1 * wide, LANES), wide)].reshape(-1, wide)
+
+    def out_place(ref):
+        unit = ref.shape[1] // nz
+        return lambda z1: ref.at[:, pl.ds(pl.multiple_of(z1 * unit, LANES), unit)]
+
+    makers = (
+        lambda s1: turn_first(columns(n2, s1), d_gate[...]),
+        lambda s1: turn_first(columns(n2, s1), d_up[...]),
+        lambda s1: turn_first(columns(cot, s1), act[...]),
+    )
+    rets = [
+        Return(at, sends, makers[i], room, refs.take(2), out_place(ffn_out[i]), refs.take(n_ret))
+        for i, room in enumerate((gate_w, up_w, down_w))
+    ]
+
+    def summed(make, first, cols):
+        room = wa.at[:, :, pl.ds(first, cols)]
+        ret = Return(at, sends, make, room, refs.take(2), None, refs.take(n_ret))
+        (land,) = refs.take(1)
+        ret.chain = ChainSum(at, sends, (ret.piece, land), refs.take(n_sum))
+        return ret
+
+    r_qkv = summed(lambda s1: turn_first(columns(normed1_b, s1), d_projb[...]), 0, qkv_cols)
+    r_out = summed(lambda s1: turn_first(columns(d_resid_b, s1), attn[...]), qkv_cols, q_cols)
+    r_dn2, r_ffn = (
+        Reduce(at, sends, parts, refs.take(3), refs.take(n_red)) for parts in (dn2_part, ffn_part)
+    )
+    (d_resid_f, d_attn, d_score, dkv, dkv_land, dn1_part, dn1_land, small_b, small_land, small_z,
+     small_zland, small_y, small_yland, dkvs, dkvr, shs, shr, szs, szr, ysems, yrecv) = refs.take(21)
+
+    at.greet(everyone=True)
     w_small.over_z()
     w_small.own_block()
     w_attn.over_z()
     w_attn.own_block()
-    ffn[0].over_z()
-    ffn[0].own_block()
     my_half = cot_in.at[pl.ds(pl.multiple_of(at.y * half, SUBLANES), half)]
     sends.here(cot_in.at[pl.ds(0, half)], cot.at[at.z, 0], cot_sem.at[0])
     sends.here(cot_in.at[pl.ds(half, half)], cot.at[at.z, 1], cot_sem.at[1])
+    w_small.pass_z()
+    w_attn.pass_z()
+    ffn[0].over_z()
+    for item in ffn:
+        item.own_block()
 
     hidden_f = hidden[...].astype(F32)
     factor1 = lax.rsqrt(jnp.mean(hidden_f * hidden_f, axis=1, keepdims=True) + EPSILON)
-    w_small.pass_all()
-    w_attn.pass_all()
+    w_small.pass_s()
+    w_attn.pass_s()
     w_small.finish()
     gains = whole_lines(small, ns * nz, depth)
-    lines[...] = gains
-    normed1 = (hidden[...].astype(F32) * factor1 * gains[0:1, :]).astype(BF16)
-    w_attn.finish()
-
+    normed1_b[...] = (hidden[...].astype(F32) * factor1 * gains[0:1, :]).astype(BF16)
     width_each = HD // (ns * nz)
     lane = lax.broadcasted_iota(jnp.int32, (8, LANES), 1)
     bias = jnp.zeros((8, LANES), F32)
@@ -316,13 +649,12 @@
         line = small[b, 8:16, :].astype(F32)
         moved = pltpu.roll(line, b * width_each, 1) if b else line
         bias = jnp.where((lane >= b * width_each) & (lane < (b + 1) * width_each), moved, bias)
+    w_attn.finish()
     cos_t, sin_t = cosine[...], sine[...]
 
     def projected(head):
-        part = jnp.dot(
-            normed1, wa[:, head * HD:(head + 1) * HD], preferred_element_type=F32
-        )
-        return part + bias[head:head + 1, :]
+        weight = wa[:, :, head * HD:(head + 1) * HD].reshape(width, HD)
+        return jnp.dot(normed1_b[...], weight, preferred_element_type=F32) + bias[head:head + 1, :]
 
     def rotated(values):
         return values * cos_t + pltpu.roll(values, HD // 2, 1) * sin_t
@@ -331,29 +663,25 @@
         kv_all[at.z, :, j * HD:(j + 1) * HD] = rotated(projected(heads + j)).astype(BF16)
         kv_all[at.z, :, (kv + j) * HD:(kv + j + 1) * HD] = projected(heads + kv + j).astype(BF16)
     for d in range(1, nz):
-        sends.go(kv_all.at[at.z], kv_all.at[at.z], kvs.at[d], kvr.at[d], context=at.z_to(d))
+        z2 = at.z_to(d)
+        sends.go(kv_all.at[at.z], kv_all.at[at.z], kvs.at[z2], kvr.at[at.z], context=z2)
     ffn[1].over_z()
-    ffn[1].own_block()
+    ffn[2].over_z()
     t_cot.over_z(my_half)
-    ffn[0].pass_all()
     for h in range(heads):
         query[:, h * HD:(h + 1) * HD] = rotated(projected(h)).astype(BF16)
+    ffn[0].pass_z()
     for d in range(1, nz):
-        src = kv_all.at[at.z_from(d)]
-        landed(src, kvs.at[d], kvr.at[d], context=at.z_from(d))
-
-    scale = HD ** (-0.5)
-    group_rows = nz * rows
+        z1 = at.z_from(d)
+        landed(kv_all.at[z1], kvs.at[z1], kvr.at[z1], context=z1)
+
+    def keys_of(j):
+        return kv_all[:, :, j * HD:(j + 1) * HD].reshape(group_rows, HD)
+
     keep = mask[...] > 0
-    repeat = heads // kv
     for h in range(heads):
-        j = h // repeat
-        keys = kv_all[:, :, j * HD:(j + 1) * HD].reshape(group_rows, HD)
-        values = kv_all[:, :, (kv + j) * HD:(kv + j + 1) * HD].reshape(group_rows, HD)
-        scores = lax.dot_general(
-            query[:, h * HD:(h + 1) * HD], keys, (((1,), (1,)), ((), ())),
-            preferred_element_type=F32,
-        )
+        keys, values = keys_of(h // repeat), keys_of(kv + h // repeat)
+        scores = turn_last(query[:, h * HD:(h + 1) * HD], keys)
         scores = jnp.where(keep, scores * scale, -1e30)
         peak = jnp.max(scores, axis=1, keepdims=True)
         lse = peak + jnp.log(jnp.sum(jnp.exp(scores - peak), axis=1, keepdims=True))
@@ -361,18 +689,12 @@
         probs[h * rows:(h + 1) * rows, :] = p
         out = jnp.dot(p.astype(BF16), values, preferred_element_type=F32)
         attn[:, h * HD:(h + 1) * HD] = out.astype(BF16)
-    part = lax.dot_general(
-        attn[...], wa[:, qkv_cols:qkv_cols + q_cols], (((1,), (1,)), ((), ())),
-        preferred_element_type=F32,
-    ).astype(BF16)
+    out_w = wa[:, :, qkv_cols:qkv_cols + q_cols].reshape(width, q_cols)
+    part = turn_last(attn[...], out_w).astype(BF16)
     ypart[0] = part[:half]
     ypart[1] = part[half:]
     sends.go(ypart.at[at.twin], yland, yps, ypr, tensor=at.twin)
-    ffn[2].over_z()
-    ffn[2].own_block()
-    for d in range(1, nz):
-        t_cot.pass_z(d)
-    ffn[1].pass_all()
+    ffn[0].pass_s()
 
     landed(yland, yps, ypr, tensor=at.twin)
     base = pl.multiple_of(at.y * half, SUBLANES)
@@ -382,53 +704,253 @@
     factor2 = lax.rsqrt(jnp.mean(res * res, axis=1, keepdims=True) + EPSILON)
     n2[at.z, at.y] = (res * factor2 * gains[1:2, :]).astype(BF16)
     t_n2.over_z(n2.at[at.z, at.y])
-    t_n2.over_y(0, n2.at[at.z, at.y])
-    for d in range(1, nz):
-        t_n2.pass_z(d)
-    ffn[2].pass_all()
-    for d in range(nz):
-        t_n2.wait_y(d)
-    for d in range(1, nz):
-        t_cot.wait_y(d)
+    t_n2.over_y(at.z, n2.at[at.z, at.y])
+    ffn[1].pass_z()
+    ffn[1].pass_s()
+    ffn[2].pass_z()
+    t_cot.pass_z()
+    t_n2.pass_z()
+    ffn[2].pass_s()
+    t_cot.wait_y(range(nz), lambda z1: at.z != z1)
     for item in ffn:
         item.finish()
+    for copy in sends.local:
+        copy.wait()
+    sends.local = []
+
+    def weight(ref):
+        return ref[...].reshape(width, -1)
+
+    d_act[...] = jnp.dot(cot[...].reshape(group_rows, width), weight(down_w), preferred_element_type=F32)
+    few, tall = nz // 2, 32
+    chunk = few * rows
+
+    def half_block(first):
+        t_n2.wait_y([first * few + i for i in range(few)])
+        start = pl.multiple_of(first * chunk, chunk)
+        mine = n2[pl.ds(first * few, few)].reshape(chunk, width)
+        gate[...] = jnp.dot(mine, weight(gate_w), preferred_element_type=F32)
+        up_val[...] = jnp.dot(mine, weight(up_w), preferred_element_type=F32)
+
+        @pl.loop(0, chunk // tall)
+        def _(i):
+            line = pl.ds(pl.multiple_of(i * tall, tall), tall)
+            whole = pl.ds(pl.multiple_of(start + i * tall, tall), tall)
+            g, u, d = gate[line, :], up_val[line, :], d_act[whole, :]
+            sigma = jax.nn.sigmoid(g)
+            silu_val = g * sigma
+            act[whole, :] = (silu_val * u).astype(BF16)
+            d_gate[whole, :] = (d * u * sigma * (1.0 + g * (1.0 - sigma))).astype(BF16)
+            d_up[whole, :] = (d * silu_val).astype(BF16)
+
+        span = pl.ds(start, chunk)
+        dn2_part[pl.ds(first * few, few)] = (
+            turn_last(d_gate[span, :], weight(gate_w)) + turn_last(d_up[span, :], weight(up_w))
+        ).astype(BF16).reshape(few, 2, half, width)
+        r_dn2.over_y([first * few + i for i in range(few)])
+
+    nearer = lax.div(at.z, few)
+    half_block(nearer)
+    half_block(1 - nearer)
+    w_sends.drain()
+
+    rets[0].give_all()
+    rets[0].over_s()
+    r_dn2.pass_y()
+    rets[1].give_all()
+    rets[1].over_s()
+    res = resid[...]
+    factor2 = lax.rsqrt(jnp.mean(res * res, axis=1, keepdims=True) + EPSILON)
+    unit2 = res * factor2
+    dn2 = r_dn2.total()
+    grad_g2 = jnp.sum(dn2 * unit2, axis=0, keepdims=True)
+    scaled = dn2 * gains[1:2, :]
+    back2 = factor2 * (scaled - unit2 * jnp.mean(scaled * unit2, axis=1, keepdims=True))
+    d_res = cot[at.z, at.y].astype(F32) + back2
+    d_resid_f[at.y] = d_res
+    d_resid_b[at.y] = d_res.astype(BF16)
+    mine_b, mine_f = d_resid_b.at[at.y], d_resid_f.at[at.y]
+    sends.go(mine_b, mine_b, ysems.at[0], yrecv.at[0], tensor=at.twin)
+    ffn_part[...] = turn_last(act[...], weight(down_w)).astype(BF16).reshape(nz, 2, half, width)
+    rets[2].give_all()
+    rets[0].over_z_all()
+    landed(d_resid_b.at[at.twin], ysems.at[0], yrecv.at[0], tensor=at.twin)
+    r_ffn.over_y(far_first(nz))
+    sends.go(mine_f, mine_f, ysems.at[1], yrecv.at[1], tensor=at.twin)
+
+    d_resid_all = d_resid_b[...].reshape(rows, width)
+    out_w = wa[:, :, qkv_cols:qkv_cols + q_cols].reshape(width, q_cols)
+    d_attn[...] = jnp.dot(d_resid_all, out_w, preferred_element_type=F32).astype(BF16)
+    r_out.give_all()
+    r_out.over_s()
+
+    def unrotated(values):
+        return values * cos_t - pltpu.roll(values, HD // 2, 1) * sin_t
+
+    bias_rows = [None] * (heads + 2 * kv)
+
+    def place(head, grad):
+        bias_rows[head] = jnp.sum(grad, axis=0, keepdims=True)
+        d_projb[:, head * HD:(head + 1) * HD] = grad.astype(BF16)
+
+    for j in range(kv):
+        keys, values = keys_of(j), keys_of(kv + j)
+        d_values = jnp.zeros((group_rows, HD), F32)
+        d_keys = jnp.zeros((group_rows, HD), F32)
+        for h in range(j * repeat, (j + 1) * repeat):
+            d_out = d_attn[:, h * HD:(h + 1) * HD]
+            p = probs[h * rows:(h + 1) * rows, :]
+            d_prob = turn_last(d_out, values)
+            delta = jnp.sum(
+                d_out.astype(F32) * attn[:, h * HD:(h + 1) * HD].astype(F32), axis=1, keepdims=True
+            )
+            d_score[...] = (p * (d_prob - delta)).astype(BF16)
+            d_query = jnp.dot(d_score[...], keys, preferred_element_type=F32)
+            place(h, unrotated(d_query * scale))
+            d_keys = d_keys + turn_first(d_score[...], query[:, h * HD:(h + 1) * HD])
+            d_values = d_values + turn_first(p.astype(BF16), d_out)
+        for i, grad in ((j, d_keys * scale), (kv + j, d_values)):
+            dkv[:, :, i * HD:(i + 1) * HD] = grad.astype(BF16).reshape(nz, rows, HD)
+    for d in range(1, nz):
+        z2 = at.z_to(d)
+        sends.go(dkv.at[z2], dkv_land.at[at.z], dkvs.at[z2], dkvr.at[at.z], context=z2)
+    rets[1].over_z_all()
+    d_own = dkv[at.z].astype(F32)
+    for d in range(1, nz):
+        z1 = at.z_from(d)
+        landed(dkv_land.at[z1], dkvs.at[z1], dkvr.at[z1], context=z1)
+        d_own = d_own + dkv_land[z1].astype(F32)
+    for j in range(kv):
+        place(heads + j, unrotated(d_own[:, j * HD:(j + 1) * HD]))
+        place(heads + kv + j, d_own[:, (kv + j) * HD:(kv + j + 1) * HD])
+    qkv_w = wa[:, :, :qkv_cols].reshape(width, qkv_cols)
+    dn1_part[...] = turn_last(d_projb[...], qkv_w).astype(BF16)
+    sends.go(dn1_part, dn1_land, ysems.at[2], yrecv.at[2], tensor=at.twin)
+    r_qkv.give_all()
+    r_qkv.over_s()
+    rets[2].over_s()
+    r_ffn.pass_y()
+    r_out.over_z_all()
+
+    block_out[at.y] = (r_ffn.total() + resid[...]).astype(BF16)
+    sends.go(block_out.at[at.y], block_out.at[at.y], ysems.at[3], yrecv.at[3], tensor=at.twin)
+
+    landed(dn1_land, ysems.at[2], yrecv.at[2], tensor=at.twin)
+    landed(d_resid_f.at[at.twin], ysems.at[1], yrecv.at[1], tensor=at.twin)
+    dn1 = dn1_part[...].astype(F32) + dn1_land[...].astype(F32)
+    hidden_f = hidden[...].astype(F32)
+    factor1 = lax.rsqrt(jnp.mean(hidden_f * hidden_f, axis=1, keepdims=True) + EPSILON)
+    unit1 = hidden_f * factor1
+    row = lax.broadcasted_iota(jnp.int32, (rows, 1), 0)
+    my_row = (row >= at.y * half) & (row < (at.y + 1) * half)
+    grad_g1 = jnp.sum(jnp.where(my_row, dn1 * unit1, 0.0), axis=0, keepdims=True)
+    scaled = dn1 * gains[0:1, :]
+    back1 = factor1 * (scaled - unit1 * jnp.mean(scaled * unit1, axis=1, keepdims=True))
+    input_grad[...] = d_resid_f[...].reshape(rows, width) + back1
+
+    both = jnp.concatenate([grad_g1, grad_g2, jnp.zeros((6, width), F32)], axis=0)
+    bias = jnp.concatenate(bias_rows, axis=0)
+    for b in range(ns * nz):
+        moved = pltpu.roll(bias, LANES - b * width_each, 1) if b else bias
+        small_b[b // nz, b % nz] = jnp.concatenate([piece_of_lines(both, b, depth), moved], axis=0)
+    for k in range(1, ns):
+        s2 = lax.rem(at.s + k, ns)
+        sends.go(small_b.at[s2], small_land.at[k], shs.at[k], shr.at[k], shard=s2)
+    r_qkv.over_z_all()
+    total = small_b[at.s]
+    for k in range(1, ns):
+        s1 = lax.rem(at.s - k + ns, ns)
+        landed(small_land.at[k], shs.at[k], shr.at[k], shard=s1)
+        total = total + small_land[k]
+    small_z[...] = total
+    for d in range(1, nz):
+        sends.go(small_z.at[at.z_to(d)], small_zland.at[d], szs.at[d], szr.at[d], context=at.z_to(d))
+    rets[2].over_z_all()
+    total = small_z[at.z]
+    for d in range(1, nz):
+        landed(small_zland.at[d], szs.at[d], szr.at[d], context=at.z_from(d))
+        total = total + small_zland[d]
+    small_y[...] = total
+    sends.go(small_y, small_yland, ysems.at[4], yrecv.at[4], tensor=at.twin)
+    out_grad[...] = r_out.chain.total(r_out.piece(at.z)[...].astype(F32))
+    qkv_grad[...] = r_qkv.chain.total(r_qkv.piece(at.z)[...].astype(F32))
+    landed(small_yland, ysems.at[4], yrecv.at[4], tensor=at.twin)
+    small_out[:8, :] = small_y[:8, :] + small_yland[:8, :]
+    small_out[8:, :] = small_y[8:, :]
+    landed(block_out.at[at.twin], ysems.at[3], yrecv.at[3], tensor=at.twin)
+    for ret in rets:
+        ret.finish()
     sends.drain()
 
 
-def front(ns, nz, heads, kv, wa_in, small_in, ffn_in, hidden, cot, cosine, sine, mask):
+def layer(ns, nz, heads, kv, wa_in, small_in, ffn_in, hidden, cot, cosine, sine, mask):
     rows, width = hidden.shape
-    owners = ns * nz
-    half = rows // 2
+    owners, half, group_rows = ns * nz, rows // 2, nz * rows
+    depth, cols = wa_in.shape
     unit = ffn_in[0].shape[2]
-    wide = owners * wa_in.shape[0]
+    q_cols, kv_cols = heads * HD, 2 * kv * HD
+    qkv_cols = q_cols + kv_cols
     dma = pltpu.SemaphoreType.DMA
     shape = jax.ShapeDtypeStruct
+    room = pltpu.VMEM
     vmem = pl.BlockSpec(memory_space=pltpu.VMEM)
     anyspace = pl.BlockSpec(memory_space=pl.ANY)
+    scratch = [room((ns, nz * depth, cols), BF16)] + [room((ns, nz * depth, unit), BF16)] * 3
+    scratch += [
+        room((owners, 16, LANES), BF16),
+        room((2, half, width), BF16),
+        room((half, width), BF16),
+        room((nz, 2, half, width), BF16),
+        room((nz, 2, half, width), BF16),
+        room((half, width), F32),
+        room((rows, q_cols), BF16),
+        room((nz, rows, kv_cols), BF16),
+        room((heads * rows, group_rows), F32),
+        room((rows, q_cols), BF16),
+    ]
+    scratch += Spread.sems(ns, nz) * 5 + Tokens.sems(nz) * 2
+    scratch += [dma((nz,)), dma((nz,)), dma, dma, dma((2,))]
+    scratch += [room((group_rows // 2, unit), F32)] * 2 + [room((group_rows, unit), F32)]
+    scratch += [room((group_rows, unit), BF16)] * 3 + [room((nz, 2, half, width), BF16)] * 2
+    scratch += [
+        room((rows, width), BF16), room((2, half, width), BF16), room((rows, qkv_cols), BF16),
+    ]
+    for _ in range(3):
+        scratch += Return.lands(ns, nz, depth, unit) + Return.sems(ns, nz)
+    for n in (qkv_cols, q_cols):
+        scratch += Return.lands(ns, nz, depth, n) + Return.sems(ns, nz)
+        scratch += ChainSum.bufs(nz, (depth, n))[1:] + ChainSum.sems(nz)
+    for _ in range(2):
+        scratch += Reduce.bufs(nz, half, width) + Reduce.sems(nz)
+    scratch += [
+        room((2, half, width), F32),
+        room((rows, q_cols), BF16),
+        room((rows, group_rows), BF16),
+        room((nz, rows, kv_cols), BF16),
+        room((nz, rows, kv_cols), BF16),
+        room((rows, width), BF16),
+        room((rows, width), BF16),
+        room((ns, nz, 16, LANES), F32),
+        room((ns, nz, 16, LANES), F32),
+        room((nz, 16, LANES), F32),
+        room((nz, 16, LANES), F32),
+        room((16, LANES), F32),
+        room((16, LANES), F32),
+        dma((nz,)), dma((nz,)), dma((ns,)), dma((ns,)), dma((nz,)), dma((nz,)), dma((5,)), dma((5,)),
+    ]
     return pl.pallas_call(
-        functools.partial(front_kernel, ns, nz, heads, kv),
+        functools.partial(layer_kernel, ns, nz, heads, kv),
         out_shape=[
-            shape((wide, wa_in.shape[1]), BF16),
-            *[shape((wide, unit), BF16)] * 3,
-            shape((8, wide), F32),
-            shape((nz, 2, half, width), BF16),
-            shape((nz, 2, half, width), BF16),
-            shape((half, width), F32),
-            shape((rows, heads * HD), BF16),
-            shape((nz, rows, 2 * kv * HD), BF16),
-            shape((heads * rows, nz * rows), F32),
-            shape((rows, heads * HD), BF16),
+            shape((2, half, width), BF16),
+            shape((rows, width), F32),
+            shape((depth, qkv_cols), F32),
+            shape((depth, q_cols), F32),
+            shape((16, LANES), F32),
+            *[shape((depth, nz * unit), BF16)] * 3,
         ],
         in_specs=[anyspace] * 5 + [vmem, anyspace] + [vmem] * 3,
-        out_specs=[vmem] + [anyspace] * 3 + [vmem] * 8,
-        scratch_shapes=[
-            pltpu.VMEM((owners, 16, LANES), BF16),
-            pltpu.VMEM((2, half, width), BF16),
-            pltpu.VMEM((half, width), BF16),
-        ]
-        + Spread.sems(ns, nz) * 5
-        + Tokens.sems(nz) * 2
-        + [dma((nz,)), dma((nz,)), dma, dma, dma((2,))],
+        out_specs=[vmem] * 5 + [anyspace] * 3,
+        scratch_shapes=scratch,
         compiler_params=pltpu.CompilerParams(
             collective_id=0, has_side_effects=True, vmem_limit_bytes=VMEM_BYTES
         ),
@@ -455,15 +977,9 @@
     parts = 2
     heads = H // parts
     kv = KVH // parts
-    repeat = heads // kv
-    scale = HD ** (-0.5)
     block_index = lax.axis_index("context")
-    part_index = lax.axis_index("tensor")
-    half_rows = rows // parts
     unit_cols = -(-hidden_units // (nz * LANES)) * LANES
     padded = unit_cols * nz
-    q_cols = heads * HD
-    k_cols = kv * HD
 
     def by_place(weight):
         full = jnp.pad(weight, ((0, 0), (0, padded - hidden_units)))
@@ -487,98 +1003,25 @@
     )
     cosine, sine = rotary_tables(index_local - earlier)
 
-    wa, gate_full, up_full, down_full, lines, n2, cot, resid_half, query, kv_all, p_soft, attn = front(
+    block_out, input_grad, grad_qkv, grad_out, small, grad_gate, grad_up, grad_down = layer(
         ns, nz, heads, kv, wa_in, small_in, ffn_in, hidden_in, out_cotangent, cosine, sine,
         allowed.astype(F32),
     )
-    gain_one, gain_two = lines[0], lines[1]
-    qkv_full = wa[:, : q_cols + 2 * k_cols]
-    out_full = wa[:, q_cols + 2 * k_cols :]
-    normed2 = n2.reshape(group_rows, width)
-    cot = cot.reshape(group_rows, width)
-    hidden_f = hidden_in.astype(F32)
-    normed1, unit1, factor1 = norm_forward(hidden_f, gain_one)
-    _, unit2, factor2 = norm_forward(resid_half, gain_two)
-    query = jnp.transpose(query.reshape(rows, heads, HD), (1, 0, 2)).reshape(kv, repeat * rows, HD)
-    kv_rows = kv_all.reshape(group_rows, 2 * kv, HD)
-    keys = jnp.transpose(kv_rows[:, :kv], (1, 0, 2))
-    values = jnp.transpose(kv_rows[:, kv:], (1, 0, 2))
-    p_soft = p_soft.reshape(kv, repeat * rows, group_rows)
-    probs = p_soft.astype(BF16)
-    outs = jnp.transpose(attn.reshape(rows, heads, HD), (1, 0, 2)).reshape(kv, repeat * rows, HD)
-    mine = part_index * half_rows
-    cot_half = lax.dynamic_slice_in_dim(out_cotangent, mine, half_rows)
-    blocks = nz
-    gate = dot(normed2, gate_full)
-    up_val = dot(normed2, up_full)
-    sigma = jax.nn.sigmoid(gate)
-    silu_val = gate * sigma
-    act = (silu_val * up_val).astype(BF16)
-    ffn_part = contract_last(act, down_full).astype(BF16)
-    d_act = dot(cot, down_full)
-    d_gate = (d_act * up_val * sigma * (1.0 + gate * (1.0 - sigma))).astype(BF16)
-    d_up = (d_act * silu_val).astype(BF16)
-    dn2_part = (contract_last(d_gate, gate_full) + contract_last(d_up, up_full)).astype(BF16)
-    ffn_half = lax.psum_scatter(ffn_part, TEAM, scatter_dimension=0, tiled=True)
-    block_half = (resid_half + ffn_half.astype(F32)).astype(BF16)
-    block_out = lax.all_gather(block_half, "tensor", axis=0, tiled=True)
-    dn2_half = lax.psum_scatter(dn2_part, TEAM, scatter_dimension=0, tiled=True).astype(F32)
-    grad_g2, d_back2 = norm_backward(dn2_half, unit2, factor2, gain_two)
-    d_resid_half = cot_half.astype(F32) + d_back2
-
-    def give_back(grad):
-        part = lax.psum_scatter(grad.astype(BF16), "shard", scatter_dimension=0, tiled=True)
-        part = part.reshape(blocks, depth, unit_cols)
-        part = lax.all_to_all(part, "context", split_axis=0, concat_axis=2, tiled=True)
-        return part.reshape(depth, padded)[:, :hidden_units].astype(F32)
-
-    sum_gate = give_back(contract_first(normed2, d_gate))
-    sum_up = give_back(contract_first(normed2, d_up))
-    sum_down = give_back(contract_first(cot, act)).T
-
-    d_resid_b = lax.all_gather(d_resid_half.astype(BF16), "tensor", axis=0, tiled=True)
-    grad_out = contract_first(d_resid_b, attn)
-    d_attn = dot(d_resid_b, out_full).astype(BF16)
-    d_outs = jnp.transpose(d_attn.reshape(rows, heads, HD), (1, 0, 2)).reshape(
-        kv, repeat * rows, HD
-    )
-    d_prob = batched(d_outs, values, 2, 2)
-    delta = jnp.sum(d_outs.astype(F32) * outs.astype(F32), axis=2, keepdims=True)
-    d_score = (p_soft * (d_prob - delta)).astype(BF16)
-    d_query = batched(d_score, keys, 2, 1) * scale
-    d_keys = batched(d_score, query, 1, 1) * scale
-    d_values = batched(probs, d_outs, 1, 1)
-    d_kv = jnp.concatenate([d_keys, d_values], axis=0).astype(BF16)
-    d_kv = lax.psum_scatter(d_kv, "context", scatter_dimension=1, tiled=True).astype(F32)
-    d_query = unrotate(d_query.reshape(heads, rows, HD), cosine, sine)
-    d_keys = unrotate(d_kv[:kv], cosine, sine)
-    d_proj = jnp.transpose(jnp.concatenate([d_query, d_keys, d_kv[kv:]], axis=0), (1, 0, 2))
-    grad_bias = jnp.sum(d_proj, axis=0)
-    d_projb = d_proj.reshape(rows, -1).astype(BF16)
-    grad_qkv = contract_first(normed1, d_projb)
-    dn1_part = contract_last(d_projb, qkv_full).astype(BF16)
-    dn1_half = lax.psum_scatter(dn1_part, "tensor", scatter_dimension=0, tiled=True).astype(F32)
-    unit1_half = lax.dynamic_slice_in_dim(unit1, mine, half_rows)
-    factor1_half = lax.dynamic_slice_in_dim(factor1, mine, half_rows)
-    grad_g1, d_back1 = norm_backward(dn1_half, unit1_half, factor1_half, gain_one)
-    input_grad = lax.all_gather(d_resid_half + d_back1, "tensor", axis=0, tiled=True)
-
-    gains = lax.psum(jnp.stack([grad_g1, grad_g2]), "tensor")
-    sum_gains = lax.psum_scatter(gains, OWNERS, scatter_dimension=1, tiled=True)
-    sum_qkv = lax.psum_scatter(grad_qkv.astype(BF16), OWNERS, scatter_dimension=0, tiled=True)
-    sum_bias = lax.psum_scatter(grad_bias, OWNERS, scatter_dimension=1, tiled=True)
-    sum_out = lax.psum_scatter(grad_out.astype(BF16), OWNERS, scatter_dimension=0, tiled=True)
+
+    def all_columns(grad):
+        return grad[:, :hidden_units].astype(F32)
+
     return (
-        block_out,
+        block_out.reshape(rows, width),
         input_grad,
-        sum_gains[0],
-        sum_qkv.astype(F32),
-        sum_bias,
-        sum_out.astype(F32).T,
-        sum_gains[1],
-        sum_gate,
-        sum_up,
-        sum_down,
+        small[0, :depth],
+        grad_qkv,
+        small[8:, : qkv_bias.shape[1]],
+        grad_out.T,
+        small[1, :depth],
+        all_columns(grad_gate),
+        all_columns(grad_up),
+        all_columns(grad_down).T,
     )
 
 
@@ -751,7 +1194,7 @@
 
     def local(*args):
         depth = args[7].shape[0]
-        if depth % SUBLANES == 0 and ns % 2 == 0 and ns > 2 and nz > 1 and parts == 2:
+        if depth % SUBLANES == 0 and ns % 2 == 0 and ns > 2 and nz % 2 == 0 and parts == 2:
             return fast_step(ns, nz, *args)
         return general_step(*args)
 

time: 756 us -> 309 us (0.41)
  waiting for transfers between devices: 399 us -> 0 us
  Pallas kernels: 157 us -> 285 us
  blocking collectives: 66.8 us -> 0 us
  matrix products: 53.4 us -> 0 us
  starting transfers between devices: 17.8 us -> 0 us
  between operations: 15.5 us -> 0.73 us
  local copies, waits for them, and re-layouts: 19.3 us -> 9.73 us
  other arithmetic: 21.4 us -> 12.9 us
    reduce_scatter x9 -> x0, waiting for transfers between devices: 340 us -> none  [the longest x1 68.1 us: fast_step(): lax.psum_scatter(dn2_part, TEAM, scatter_dimension=0, tiled=True)]
    pallas_call x1, Pallas kernels: 157 us -> 285 us  [layer(): pl.pallas_call(functools.partial(layer_kernel, ns, nz, heads, kv), out_sh...]
    dot_general x17 -> x0, matrix products: 53.4 us -> none  [the longest x5 22.4 us: contract_first(): lax.dot_general(left, right, (((0,), (0,)), ((), ())), preferred_element_...]
    unnamed x11 -> x0, waiting for transfers between devices: 44.1 us -> none
    unnamed x1 -> x0, blocking collectives: 40.6 us -> none
    all_gather x3 -> x0, blocking collectives: 21.2 us -> none  [the longest x1 8.43 us: fast_step(): lax.all_gather(d_resid_half + d_back1, 'tensor', axis=0, tiled=True)]
    all_to_all x3 -> x0, starting transfers between devices: 17.2 us -> none  [give_back(): lax.all_to_all(part, 'context', split_axis=0, concat_axis=2, tiled=True)]
    all_to_all x3 -> x0, waiting for transfers between devices: 15.6 us -> none  [give_back(): lax.all_to_all(part, 'context', split_axis=0, concat_axis=2, tiled=True)]
  transfers between devices with their start and end apart: 13 -> 0, of which waited for: 9 -> 0; matrix products, arithmetic and copies ran while one was open for 7% -> 0% of each run, Pallas kernels for 0% -> 0%
where the time goes in v3:
time: 309 us
  Pallas kernels  285 us (92%)
  other arithmetic  12.9 us (4%)
  local copies, waits for them, and re-layouts  9.73 us (3%)
    pallas_call x1, Pallas kernels, layer(): pl.pallas_call(functools.partial(layer_kernel, ns, nz, heads, kv), out_sh...  285 us

profile of v3, /device:TPU:10, one launch (start us, length us, event | category | flops | bytes accessed | tf_op | source)
XLA Modules:
  0.0 308.8 jit_solution(18417889535716040356)
XLA Ops:
  0.6 0.0 copy-start
  0.7 0.7 dynamic-slice_bitcast_fusion
  1.4 0.9 convert_reduce_fusion
  2.3 0.7 fusion.10
  3.0 1.3 fusion.4.refs_1_
  4.2 0.3 fusion.2
  4.6 0.7 pad_maximum_fusion.2.refs_8_
  5.3 0.7 pad_maximum_fusion.1.refs_7_
  6.0 1.5 fusion.1.refs_9_
  7.5 1.8 pad_maximum_fusion.refs_0_
  9.2 0.0 copy-done
  9.2 0.0 copy-start.1
  9.2 0.1 pad.20
  9.3 0.0 copy-start.2
  9.3 1.0 copy.30
  10.3 0.3 copy-done.1
  10.6 0.1 pad.21
  10.7 0.3 copy-done.2
  11.0 0.1 pad.22
  11.1 1.3 bitcast_bitcast_fusion
  12.4 285.5 %shard_map.186 = (bf16[2,64,1536]{2,1,0:T(8,128)(2,1)}, f32[128,1536]{1,0:T(8,128)}, f32[96,1024]{1,0:T(8,128)}, f32[96,768]{1,0:T(8,128)}, f32[16,128]{1,0:T(8,...) custom-call(bf16[96,1792]{1,0:T(8,128)(2,1)} %pad_maximum_fusion.refs_0_, ...), custom_call_target="tpu_custom_call" | custom-call | tf_op jit(solution)/shard_map/pallas_call | solution.py:941
  297.9 0.0 copy-start.4
  297.9 1.3 slice_bitcast_fusion
  299.2 1.3 slice.19
  300.4 2.5 slice_convert_fusion.1
  302.9 0.0 copy-done.4
  302.9 0.0 copy-start.3
  302.9 1.3 slice_convert_fusion
  304.2 0.2 copy-done.3
  304.4 0.0 copy-start.7
  304.4 0.0 copy-start.5
  304.4 1.3 convert_bitcast_fusion
  305.7 0.0 copy-done.7
  305.7 0.0 copy-start.6
  305.7 0.0 copy-start.8
  305.7 0.7 copy.35
  306.5 0.0 copy-done.5
  306.5 0.9 copy.36
  307.4 0.0 copy-done.6
  307.4 0.7 copy.37
  308.1 0.0 copy-done.8
  308.1 0.7 copy.38
  (2 shorter events, 0.0 us)
Async XLA Ops:
  0.6 8.6 %copy-start = (bf16[96,4480]{1,0:T(8,128)(2,1)S(1)}, bf16[96,4480]{1,0:T(8,128)(2,1)}, u32[]{:S(2)}) copy-start(bf16[96,4480]{1,0:T(8,128)(2,1)} %param.18) | copy-start | bytes 2580484
  9.2 1.4 copy-start.1
  9.3 1.7 copy-start.2
  297.9 5.0 %copy-start.4 = (bf16[96,4608]{1,0:T(8,128)(2,1)S(1)}, bf16[96,4608]{1,0:T(8,128)(2,1)}, u32[]{:S(2)}) copy-start(bf16[96,4608]{1,0:T(8,128)(2,1)} %get-tuple-element.24) | copy-start | bytes 2654212
  302.9 1.5 copy-start.3
  304.4 1.3 copy-start.7
  304.4 2.1 copy-start.5
  305.7 1.6 copy-start.6
  305.7 2.4 copy-start.8
